TPU v7x, 32 devices: a whole 2x2x4 slice. The times are simulated.
32 devices in a mesh: groups: 2 (over y), img: 4 (over z), tpl: 2 (over x), sub: 2 (over core).
Axes of the slice: x: 2, y: 2, z: 4, core: 2. Of those that a mesh axis runs over, the one named last changes fastest.
Arguments:
- images: bfloat16 [2048, 4096], P(('groups', 'img', 'tpl', 'sub')), parts along dimension 0, may hold values from -48 to 48
- templates: bfloat16 [4096, 4096], P(('groups', 'tpl', 'sub')), parts along dimension 0, may hold values from -1 to 1, as said below
- group_ids: int32 [2048], P(('groups', 'img')), parts along dimension 0, may hold values from 0 to 31
- group_ctf: float32 [64], P('groups'), parts along dimension 0, may hold values from 1 to 2
- group_prec: float32 [64], P('groups'), parts along dimension 0, may hold values from 1 to 3
- log_prior: float32 [256], P('groups'), parts along dimension 0, may hold values from -4.5 to 4.5
- class_mask: int32 [256], P('groups'), parts along dimension 0, may hold values from 0 to 1
Outputs:
- class_sums: float32 [4096, 4096], P(('groups', 'tpl', 'sub'), 'img'), parts along dimension 0
- evidence: float32 [2048], P(('groups', 'img', 'tpl', 'sub')), parts along dimension 0
There are 2 independent parts, one for each index of `groups`. A program takes and returns all parts, laid end to end along the dimension named above; each array names one. Nothing has to cross between parts.
Inputs may be any that keep to these rules, and one draw needn't show every extreme that they name: `templates`: each row has unit length before rounding.
All inputs are finite; a program needn't handle non-finite values.
Results may differ from a plain program's by a relative error of at most 0.0028.
Values may be sent and summed in bfloat16 or wider, within the bound.
A program may use at most 64 MiB of HBM per device.

v0:
```python
import functools
import jax
import jax.numpy as jnp
from jax import lax
from jax.experimental import pallas as pl
from jax.experimental.pallas import tpu as pltpu
from jax.sharding import PartitionSpec as P

ROTS = 16
MASKED = -1e30
CHUNKS = 2
MESH = pl.DeviceIdType.MESH


def exchange_kernel(
    sizes, ids_in, ctf_in, prec_in, prior_in, mask_in, images, templates,
    sums_ref, evid_ref,
    ids_ref, ctf_ref, prec_ref, prior_ref, mask_ref, grid_buf, tmpl, tnorm, base, act, score, all_w, all_p, own_stat, stat,
    tmpl_sem, own_sem, a_send, a_recv, f_send, b_send, b_recv, g_send, s_send, s_recv,
    w_out, w_recv, p_own, in_sem,
):
    Z, X, C, K, H = sizes
    S = X * C
    g, z, x, c = [lax.axis_index(n) for n in ("groups", "img", "tpl", "sub")]
    s = x * C + c
    refs, nb = tnorm.shape
    classes = refs // ROTS
    r, pix = grid_buf.shape[2:]
    pb = pix // Z
    h_rows = r // H

    def xc(dx, dc):
        return lax.rem(x + dx, X), lax.rem(c + dc, C)

    def dev(zz, xx, cc):
        return (g, zz, xx, cc)

    def zoff(d):
        return lax.rem(z + d, Z)

    peers = [(dx, dc) for dx in range(X) for dc in range(C) if dx or dc]

    barrier = pltpu.get_barrier_semaphore()
    for dx, dc in peers:
        pl.semaphore_signal(barrier, inc=1, device_id=dev(z, *xc(dx, dc)), device_id_type=MESH)
    for d in range(1, Z):
        pl.semaphore_signal(barrier, inc=1, device_id=dev(zoff(d), x, c), device_id_type=MESH)

    started = []

    def local(src, dst, sem):
        cp = pltpu.make_async_copy(src, dst, sem)
        cp.start()
        return cp

    def remote(src, dst, send, recv, to):
        cp = pltpu.make_async_remote_copy(
            src_ref=src, dst_ref=dst, send_sem=send, recv_sem=recv, device_id=to, device_id_type=MESH
        )
        cp.start()
        started.append(cp)

    def arrive(dst, sem):
        pltpu.make_async_copy(dst, dst, sem).wait()

    small = [
        local(src, dst, in_sem.at[i])
        for i, (src, dst) in enumerate((
            (ids_in, ids_ref), (ctf_in, ctf_ref), (prec_in, prec_ref), (prior_in, prior_ref), (mask_in, mask_ref),
        ))
    ]
    tmpl_copy = local(templates, tmpl, tmpl_sem)
    own_copies = [local(images.at[k], grid_buf.at[k, s], own_sem.at[k]) for k in range(K)]

    pl.semaphore_wait(barrier, S - 1 + Z - 1)

    def piece(k, h, slot):
        return grid_buf.at[k, slot, pl.ds(h * h_rows, h_rows), :]

    def send_a(k, h):
        src = images.at[k, pl.ds(h * h_rows, h_rows), :]
        for dx in range(1, X):
            xx, cc = xc(dx, 0)
            remote(src, piece(k, h, s), a_send.at[k, h, dx - 1], a_recv.at[k, h, s], dev(z, xx, cc))
        for dc in range(1, C):
            xx, cc = xc(0, dc)
            remote(src, piece(k, h, s), a_send.at[k, h, X - 1 + dc - 1], a_recv.at[k, h, s], dev(z, xx, cc))

    order = [(k, h) for k in range(K) for h in range(H)]
    early = [(k, h) for k, h in order ]
    for k, h in early[:H]:
        send_a(k, h)
    for d in range(1, Z):
        zz = zoff(d)
        cols = pl.ds(pl.multiple_of(zz * pb, pb), pb)
        remote(images.at[:, :, cols], all_p.at[z, :, s], b_send.at[d - 1], b_recv.at[z, s], dev(zz, x, c))
    for k, h in early[H:]:
        send_a(k, h)

    for cp in small:
        cp.wait()
    first = s * classes
    for i in range(classes):
        rows = pl.ds(i * ROTS, ROTS)
        base[rows, :] = jnp.full((ROTS, nb), prior_ref[first + i], jnp.float32)
        act[rows, :] = jnp.full((ROTS, nb), mask_ref[first + i], jnp.int32).astype(jnp.float32)

    tmpl_copy.wait()

    @pl.loop(0, refs // 16)
    def _(i):
        rows = pl.ds(pl.multiple_of(i * 16, 16), 16)
        t = tmpl[rows, :].astype(jnp.float32)
        tnorm[rows, :] = jnp.broadcast_to(jnp.sum(t * t, axis=1, keepdims=True), (16, nb))

    all_ids = ids_ref[...]
    all_ctf = jnp.zeros(all_ids.shape, jnp.float32)
    all_prec = all_ctf
    for i in range(ctf_ref.shape[0]):
        hit = all_ids == i
        all_ctf = jnp.where(hit, ctf_ref[i], all_ctf)
        all_prec = jnp.where(hit, prec_ref[i], all_prec)

    def chunk(row, k):
        return jnp.concatenate([row[:, q * K * r + k * r : q * K * r + (k + 1) * r] for q in range(S)], axis=1)

    ctfs = [chunk(all_ctf, k) for k in range(K)]
    precs = [chunk(all_prec, k) for k in range(K)]

    def gather(k, h):
        for dx in range(1, X):
            xx, _ = xc(dx, 0)
            slot = xx * C + c
            arrive(piece(k, h, slot), a_recv.at[k, h, slot])
            for dc in range(1, C):
                _, cc = xc(0, dc)
                remote(piece(k, h, slot), piece(k, h, slot), f_send.at[k, h, dx - 1, dc - 1], a_recv.at[k, h, slot], dev(z, x, cc))

    def gathered(k):
        own_copies[k].wait()
        for h in range(H):
            for dx in range(X):
                for dc in range(1, C):
                    xx, cc = xc(dx, dc)
                    slot = xx * C + cc
                    arrive(piece(k, h, slot), a_recv.at[k, h, slot])

    p_copies = []

    def scores(k):
        pixels = grid_buf[k].reshape(nb, pix)
        raw = lax.dot_general(tmpl[...], pixels, (((1,), (1,)), ((), ())), preferred_element_type=jnp.float32)
        ctf, prec = ctfs[k], precs[k]
        values = (prec * ctf) * raw - (0.5 * prec * ctf * ctf) * tnorm[...] + base[...]
        values = jnp.where(act[...] > 0.0, values, MASKED)
        score[k] = values
        peak = jnp.max(values, axis=0, keepdims=True)
        total = jnp.sum(jnp.where(act[...] > 0.0, jnp.exp(values - peak), 0.0), axis=0, keepdims=True)
        row = lax.broadcasted_iota(jnp.int32, (8, nb), 0)
        own_stat[k] = jnp.where(row == 0, peak, total)
        for i, (dx, dc) in enumerate(peers):
            xx, cc = xc(dx, dc)
            remote(own_stat.at[k], stat.at[k, s], s_send.at[k, i], s_recv.at[k, s], dev(z, xx, cc))
        cols = pl.ds(pl.multiple_of(z * pb, pb), pb)
        p_copies.append(local(grid_buf.at[k, :, :, cols], all_p.at[z, k], p_own.at[k]))

    def w_go(k, zz, right):
        step = 1 if right else -1
        return pltpu.make_async_remote_copy(
            src_ref=all_w.at[k, zz], dst_ref=all_w.at[k, zz], send_sem=w_out.at[0 if right else 1, k, zz],
            recv_sem=w_recv.at[k, zz], device_id=dev(lax.rem(z + step + Z, Z), x, c), device_id_type=MESH,
        )

    def weights(k):
        parts = [(own_stat[k][0:1], own_stat[k][1:2])]
        for dx, dc in peers:
            xx, cc = xc(dx, dc)
            slot = xx * C + cc
            arrive(stat.at[k, slot], s_recv.at[k, slot])
            got = stat[k, slot]
            parts.append((got[0:1], got[1:2]))
        peak = functools.reduce(jnp.maximum, [p for p, _ in parts])
        total = functools.reduce(jnp.add, [t * jnp.exp(p - peak) for p, t in parts])
        evid = peak + jnp.log(total)
        mine = evid[:, 0:r]
        for q in range(1, S):
            mine = jnp.where(s == q, evid[:, q * r : (q + 1) * r], mine)
        evid_ref[:, k * r : (k + 1) * r] = mine
        post = jnp.where(act[...] > 0.0, jnp.exp(score[k] - peak), 0.0) / total
        all_w[k, z] = (post * (precs[k] * ctfs[k])).astype(jnp.bfloat16)

        @pl.when(z < Z - 1)
        def _():
            w_go(k, z, True).start()

        @pl.when(z > 0)
        def _():
            w_go(k, z, False).start()

    for k in range(K):
        late = [h for h in range(H) if (k, h) not in early]
        for h in range(H):
            if h in late or k == 0:
                gather(k, h)
        gathered(k)
        scores(k)
        if k + 1 < K:
            for h in range(H):
                if (k + 1, h) not in early:
                    send_a(k + 1, h)
            for h in range(H):
                if (k + 1, h) in early:
                    gather(k + 1, h)
            weights(k)

    def b_block(zz, slot):
        return all_p.at[zz, :, slot]

    def b_forward(zz):
        out = []
        for dx in range(1, X):
            xx, cc = xc(dx, 0)
            out.append((g_send.at[zz, dx - 1, 0], dev(z, xx, cc)))
        for dc in range(1, C):
            xx, cc = xc(0, dc)
            out.append((g_send.at[zz, X - 1, dc - 1], dev(z, xx, cc)))
        return [
            pltpu.make_async_remote_copy(
                src_ref=b_block(zz, s), dst_ref=b_block(zz, s), send_sem=sem, recv_sem=b_recv.at[zz, s],
                device_id=to, device_id_type=MESH,
            )
            for sem, to in out
        ]

    def b_second(zz):
        out = []
        for dx in range(1, X):
            xx, _ = xc(dx, 0)
            slot = xx * C + c
            for dc in range(1, C):
                _, cc = xc(0, dc)
                out.append(pltpu.make_async_remote_copy(
                    src_ref=b_block(zz, slot), dst_ref=b_block(zz, slot), send_sem=g_send.at[zz, dx - 1, dc],
                    recv_sem=b_recv.at[zz, slot], device_id=dev(z, x, cc), device_id_type=MESH,
                ))
        return out

    def both(d, fn):
        @pl.when(z - d >= 0)
        def _():
            fn(z - d, True)

        @pl.when(z + d < Z)
        def _():
            fn(z + d, False)

    def b_start(zz, right):
        arrive(b_block(zz, s), b_recv.at[zz, s])
        for cp in b_forward(zz):
            cp.start()

    weights(K - 1)

    @pl.loop(1, Z)
    def _(d):
        both(d, b_start)

    def product(zz):
        w = jnp.concatenate([all_w[k, zz] for k in range(K)], axis=1)
        p = all_p[zz].reshape(K * nb, pb)
        return jnp.dot(w, p, preferred_element_type=jnp.float32)

    for cp in p_copies:
        cp.wait()
    sums_ref[...] = product(z)

    def w_step(src, right):
        for k in range(K):
            arrive(all_w.at[k, src], w_recv.at[k, src])

            @pl.when((z < Z - 1) if right else (z > 0))
            def _():
                w_go(k, src, right).start()

    def p_step(src, right):
        for dx in range(1, X):
            xx, _ = xc(dx, 0)
            arrive(b_block(src, xx * C + c), b_recv.at[src, xx * C + c])
        for cp in b_second(src):
            cp.start()

    def add_step(src, right):
        for dx in range(X):
            for dc in range(1, C):
                xx, cc = xc(dx, dc)
                arrive(b_block(src, xx * C + cc), b_recv.at[src, xx * C + cc])
        sums_ref[...] += product(src)

    @pl.loop(1, Z + 1)
    def _(d):
        both(d, w_step)
        both(d, p_step)

        @pl.when(d > 1)
        def _():
            both(d - 1, add_step)

    for cp in started:
        cp.wait_send()

    def end_step(src, right):
        for cp in b_forward(src) + b_second(src):
            cp.wait_send()

    @pl.loop(1, Z)
    def _(d):
        both(d, end_step)

    for k in range(K):
        @pl.loop(0, Z)
        def _(d):
            @pl.when((z - d >= 0) & (z < Z - 1))
            def _():
                w_go(k, z - d, True).wait_send()

            @pl.when((z + d < Z) & (z > 0))
            def _():
                w_go(k, z + d, False).wait_send()


def exchange(mesh, images, templates, group_ids, group_ctf, group_prec, log_prior, class_mask):
    Z, X, C, K = mesh.shape["img"], mesh.shape["tpl"], mesh.shape["sub"], CHUNKS
    S = X * C
    rows, pix = images.shape
    refs = templates.shape[0]
    r = rows // K
    nb = S * r
    pb = pix // Z
    H = 2 if r % 32 == 0 else 1
    vmem = pl.BlockSpec(memory_space=pltpu.VMEM)
    anyw = pl.BlockSpec(memory_space=pl.ANY)
    dma = pltpu.SemaphoreType.DMA
    f32, bf16 = jnp.float32, jnp.bfloat16
    class_sums, evid = pl.pallas_call(
        functools.partial(exchange_kernel, (Z, X, C, K, H)),
        out_shape=(
            pltpu.VMEM((refs, pb), f32),
            pltpu.VMEM((1, rows), f32),
        ),
        in_specs=[anyw] * 7,
        out_specs=(vmem, vmem),
        scratch_shapes=[
            pltpu.VMEM((1, S * rows), jnp.int32),
            pltpu.SMEM(group_ctf.shape, f32),
            pltpu.SMEM(group_prec.shape, f32),
            pltpu.SMEM(log_prior.shape, f32),
            pltpu.SMEM(class_mask.shape, jnp.int32),
            pltpu.VMEM((K, S, r, pix), bf16),
            pltpu.VMEM((refs, pix), bf16),
            pltpu.VMEM((refs, nb), f32),
            pltpu.VMEM((refs, nb), f32),
            pltpu.VMEM((refs, nb), f32),
            pltpu.VMEM((K, refs, nb), f32),
            pltpu.VMEM((K, Z, refs, nb), bf16),
            pltpu.VMEM((Z, K, S, r, pb), bf16),
            pltpu.VMEM((K, 8, nb), f32),
            pltpu.VMEM((K, S, 8, nb), f32),
            dma(()), dma((K,)), dma((K, H, S)), dma((K, H, S)), dma((K, H, max(X - 1, 1), max(C - 1, 1))),
            dma((max(Z - 1, 1),)), dma((Z, S)), dma((Z, X, C)), dma((K, max(S - 1, 1))), dma((K, S)),
            dma((2, K, Z)), dma((K, Z)), dma((K,)), dma((5,)),
        ],
        compiler_params=pltpu.CompilerParams(
            collective_id=0, has_side_effects=True, vmem_limit_bytes=56 * 1024 * 1024
        ),
    )(group_ids.reshape(1, S * rows), group_ctf, group_prec, log_prior, class_mask, images.reshape(K, r, pix), templates)
    return class_sums, evid.reshape(rows)


def solution(mesh):
    placed = (
        P(("groups", "img", "tpl", "sub"), None),
        P(("groups", "tpl", "sub"), None),
        P(("groups", "img")),
        P("groups"),
        P("groups"),
        P("groups"),
        P("groups"),
    )
    return jax.shard_map(
        functools.partial(exchange, mesh),
        mesh=mesh,
        in_specs=placed,
        out_specs=(P(("groups", "tpl", "sub"), "img"), P(("groups", "img", "tpl", "sub"))),
        check_vma=False,
    )
```

profile of v0, /device:TPU:0, one launch (start us, length us, event | category | flops | bytes accessed | tf_op | source)
XLA Modules:
  0.0 47.5 jit_solution(838609203847837195)
XLA Ops:
  0.6 45.0 %shard_map.86 = (f32[512,1024]{1,0:T(8,128)S(1)}, f32[1,64]{1,0:T(1,128)S(1)}) custom-call(s32[1,256]{1,0:T(1,128)} %bitcast.5, f32[32]{0:T(128)} %ctf_in.1, f32[32]{0:T(128)} %prec_in.1, f32[128]{0:T(128)} %prior_in.1, s32[128]{0:T(128)} %mask_in.1, bf16[2,32,4096]{2,1,0:T(8,128)(2,1)} %bitcast.4, bf16[512,4096]{1,0:T(8,128)(2,1)} %templates.1), custom_call_target="tpu_custom_call" | custom-call | tf_op jit(solution)/shard_map/pallas_call | solution.py:344
  45.6 1.3 %copy.11 = f32[512,1024]{1,0:T(8,128)} copy(f32[512,1024]{1,0:T(8,128)S(1)} %get-tuple-element.6) | data formatting | bytes 4194304
  47.0 0.5 %copy.12 = f32[64]{0:T(128)} copy(f32[64]{0:T(128)S(1)} %bitcast.3) | data formatting | bytes 512
where the time goes:
time: 47.9 us; the launch traced here: 47.5 us
  Pallas kernels  45 us (94%)
  local copies, waits for them, and re-layouts  1.83 us (4%)
  between operations  0.64 us (1%)
    pallas_call x1, Pallas kernels, exchange(): pl.pallas_call(functools.partial(exchange_kernel, (Z, X, C, K, H)), out_s...  45 us
    unnamed x2, local copies, waits for them, and re-layouts  1.83 us

commit v1 on v0

v1 whole, which is shorter than its diff:
```python
import functools
import jax
import jax.numpy as jnp
from jax import lax
from jax.experimental import pallas as pl
from jax.experimental.pallas import tpu as pltpu
from jax.sharding import PartitionSpec as P

ROTS = 16
MASKED = -1e30
PIECES = 2
PARTS = 2
MESH = pl.DeviceIdType.MESH


def exchange_kernel(
    sizes, ids_in, ctf_in, prec_in, prior_in, mask_in, images, templates,
    sums_ref, evid_ref,
    ids_ref, ctf_ref, prec_ref, prior_ref, mask_ref, grid_buf, tmpl, tnorm, base, act, all_w, all_p, own_stat, stat, fac,
    in_sem, tmpl_sem, own_sem, c_send, c_recv, a_send, a_recv, f_send, p_send, p_recv, g_send,
    w_send, w_far, w_recv, s_send, s_recv, v_send, v_recv,
):
    Z, X, C, H, G = sizes
    S = X * C
    g, z, x, c = [lax.axis_index(n) for n in ("groups", "img", "tpl", "sub")]
    refs, nb = tnorm.shape
    classes = refs // ROTS
    rows, pix = grid_buf.shape[2:]
    pb = pix // Z
    hr = rows // H
    gr = refs // G
    s = x * C + c

    def chip(d):
        return lax.rem(x + d, X)

    def core(d):
        return lax.rem(c + d, C)

    def zoff(d):
        return lax.rem(z + d, Z)

    def dev(zz, xx, cc):
        return (g, zz, xx, cc)

    def scope(name):
        return jax.named_scope(name)

    peers = [(dx, dc) for dx in range(X) for dc in range(C) if dx or dc]
    inner = (z > 0) & (z < Z - 1)

    barrier = pltpu.get_barrier_semaphore()
    for dx, dc in peers:
        pl.semaphore_signal(barrier, inc=1, device_id=dev(z, chip(dx), core(dc)), device_id_type=MESH)
    for d in range(1, Z):
        pl.semaphore_signal(barrier, inc=1, device_id=dev(zoff(d), x, c), device_id_type=MESH)

    started = []

    def local(src, dst, sem):
        cp = pltpu.make_async_copy(src, dst, sem)
        cp.start()
        return cp

    def copy(src, dst, send, recv, to):
        return pltpu.make_async_remote_copy(
            src_ref=src, dst_ref=dst, send_sem=send, recv_sem=recv, device_id=to, device_id_type=MESH
        )

    def remote(*args):
        cp = copy(*args)
        cp.start()
        started.append(cp)

    def arrive(dst, sem):
        pltpu.make_async_copy(dst, dst, sem).wait()

    small = [
        local(src, dst, in_sem.at[i])
        for i, (src, dst) in enumerate((
            (ids_in, ids_ref), (ctf_in, ctf_ref), (prec_in, prec_ref), (prior_in, prior_ref), (mask_in, mask_ref),
        ))
    ]
    tmpl_copy = local(templates, tmpl, tmpl_sem)
    own_copy = local(images, grid_buf.at[0, c], own_sem)

    with scope("barrier"):
        pl.semaphore_wait(barrier, S - 1 + Z - 1)

    def piece(i, cc, h):
        return grid_buf.at[i, cc, pl.ds(h * hr, hr), :]

    for dc in range(1, C):
        remote(images, grid_buf.at[0, c], c_send.at[dc - 1], c_recv.at[c], dev(z, x, core(dc)))
    for h in range(H):
        for dx in range(1, X):
            remote(
                images.at[pl.ds(h * hr, hr), :], piece(X - dx, c, h), a_send.at[dx - 1, h], a_recv.at[X - dx, c, h],
                dev(z, chip(dx), c),
            )

    def p_block(zz, i, cc):
        return all_p.at[zz, i, cc]

    def p_copy(d):
        zz = zoff(d)
        cols = pl.ds(pl.multiple_of(zz * pb, pb), pb)
        return copy(images.at[:, cols], p_block(z, 0, c), p_send.at[d - 1], p_recv.at[z, 0, c], dev(zz, x, c))

    def outer(d):
        zz = zoff(d)
        return (zz == 0) | (zz == Z - 1)

    for d in range(1, Z):
        @pl.when(outer(d))
        def _():
            p_copy(d).start()

    with scope("small"):
        for cp in small:
            cp.wait()
    first = s * classes
    for i in range(classes):
        rws = pl.ds(i * ROTS, ROTS)
        base[rws, :] = jnp.full((ROTS, nb), prior_ref[first + i], jnp.float32)
        act[rws, :] = jnp.full((ROTS, nb), mask_ref[first + i], jnp.int32).astype(jnp.float32)

    factors, penalties = [], []
    for i in range(X):
        ids = ids_ref[chip(i)]
        ctf = jnp.zeros(ids.shape, jnp.float32)
        prec = ctf
        for q in range(ctf_ref.shape[0]):
            hit = ids == q
            ctf = jnp.where(hit, ctf_ref[q], ctf)
            prec = jnp.where(hit, prec_ref[q], prec)
        factors.append(prec * ctf)
        penalties.append(0.5 * prec * ctf * ctf)

    with scope("tmplw"):
        tmpl_copy.wait()

    with scope("tnorm"):
        @pl.loop(0, refs // 16)
        def _(i):
            rws = pl.ds(pl.multiple_of(i * 16, 16), 16)
            t = tmpl[rws, :].astype(jnp.float32)
            tnorm[rws, :] = jnp.broadcast_to(jnp.sum(t * t, axis=1, keepdims=True), (16, nb))

    def w_part(i, zz, q):
        return all_w.at[i, zz, pl.ds(q * gr, gr), :]

    def w_go(i, zz, q, right):
        step = 1 if right else -1
        return copy(
            w_part(i, zz, q), w_part(i, zz, q), w_send.at[0 if right else 1, i, zz, q], w_recv.at[i, zz, q],
            dev(lax.rem(z + step + Z, Z), x, c),
        )

    def w_two(i, q):
        zz = lax.rem(jnp.where(z == 0, z + 2, z - 2) + Z, Z)
        return copy(w_part(i, z, q), w_part(i, z, q), w_far.at[i, q], w_recv.at[i, z, q], dev(zz, x, c))

    has_two = ((z == 0) | (z == Z - 1)) if Z > 2 else None

    def forwards(src, right):
        if right:
            return (z < Z - 1) & ((src > 0) | (z != 1))
        return (z > 0) & ((src < Z - 1) | (z != Z - 2))

    def sides(d, fn):
        @pl.when(z - d >= 0)
        def _():
            fn(z - d, True)

        @pl.when(z + d < Z)
        def _():
            fn(z + d, False)

    def w_forward(i):
        def fn(src, right):
            @pl.when(forwards(src, right))
            def _():
                for q in range(G):
                    with scope(f"wf{i}"):
                        arrive(w_part(i, src, q), w_recv.at[i, src, q])
                    w_go(i, src, q, right).start()
        return fn

    def w_wait(i):
        def fn(src, right):
            @pl.when(jnp.logical_not(forwards(src, right)))
            def _():
                for q in range(G):
                    with scope(f"ww{i}"):
                        arrive(w_part(i, src, q), w_recv.at[i, src, q])
        return fn

    def scores(i):
        pixels = grid_buf[i].reshape(nb, pix)
        raw = lax.dot_general(tmpl[...], pixels, (((1,), (1,)), ((), ())), preferred_element_type=jnp.float32)
        live = act[...] > 0.0
        values = jnp.where(live, factors[i] * raw - penalties[i] * tnorm[...] + base[...], MASKED)
        peak = jnp.max(values, axis=0, keepdims=True)
        terms = jnp.where(live, jnp.exp(values - peak), 0.0)
        all_w[i, z] = terms.astype(jnp.bfloat16)
        total = jnp.sum(terms, axis=0, keepdims=True)
        row = lax.broadcasted_iota(jnp.int32, (8, nb), 0)
        own_stat[chip(i)] = jnp.where(row == 0, peak, total)
        for q in range(G):
            if Z > 2:
                @pl.when(has_two)
                def _():
                    w_two(i, q).start()

            @pl.when(z < Z - 1)
            def _():
                w_go(i, z, q, True).start()

            @pl.when(z > 0)
            def _():
                w_go(i, z, q, False).start()

    def p_forward(zz):
        out = []
        for dx in range(1, X):
            out.append(copy(p_block(zz, 0, c), p_block(zz, X - dx, c), g_send.at[zz, dx - 1, 0], p_recv.at[zz, X - dx, c], dev(z, chip(dx), c)))
        for dc in range(1, C):
            out.append(copy(p_block(zz, 0, c), p_block(zz, 0, c), g_send.at[zz, X - 1, dc - 1], p_recv.at[zz, 0, c], dev(z, x, core(dc))))
        return out

    def p_second(zz):
        out = []
        for dx in range(1, X):
            for dc in range(1, C):
                out.append(copy(p_block(zz, dx, c), p_block(zz, dx, c), g_send.at[zz, dx - 1, dc], p_recv.at[zz, dx, c], dev(z, x, core(dc))))
        return out

    def p_start(zz, right):
        with scope("pst"):
            arrive(p_block(zz, 0, c), p_recv.at[zz, 0, c])
        for cp in p_forward(zz):
            cp.start()

    def gather(dx, h):
        with scope(f"gath{h}"):
            arrive(piece(dx, c, h), a_recv.at[dx, c, h])
        for dc in range(1, C):
            remote(piece(dx, c, h), piece(dx, c, h), f_send.at[dx - 1, h, dc - 1], a_recv.at[dx, c, h], dev(z, x, core(dc)))

    own_copy.wait()
    with scope("own"):
        for dc in range(1, C):
            arrive(grid_buf.at[0, core(dc)], c_recv.at[core(dc)])
    with scope("sc0"):
        scores(0)
    for d in range(1, Z):
        @pl.when(jnp.logical_not(outer(d)))
        def _():
            p_copy(d).start()

    early = min(2, Z - 1)
    for dx in range(1, X):
        for h in range(H):
            gather(dx, h)
            if dx == 1 and h == 0:
                sides(1, w_forward(0))

                @pl.when(jnp.logical_not(inner))
                def _():
                    for d in range(1, early + 1):
                        sides(d, p_start)
            elif h == H - 1:
                for d in range(2 if dx == 1 else 1, early + 1):
                    sides(d, w_forward(dx - 1))
        with scope(f"arrA{dx}"):
            for h in range(H):
                for dc in range(1, C):
                    arrive(piece(dx, core(dc), h), a_recv.at[dx, core(dc), h])
        with scope(f"sc{dx}"):
            scores(dx)

    for i, (dx, dc) in enumerate(peers):
        remote(own_stat, stat.at[s], s_send.at[i], s_recv.at[s], dev(z, chip(dx), core(dc)))

    @pl.when(inner)
    def _():
        for d in range(1, early + 1):
            sides(d, p_start)

    @pl.loop(early + 1, Z)
    def _(d):
        sides(d, p_start)

    with scope("stat"):
        for dx, dc in peers:
            slot = chip(dx) * C + core(dc)
            arrive(stat.at[slot], s_recv.at[slot])
    for i in range(X):
        xs = chip(i)
        own = own_stat[xs]
        parts = [(own[0:1], own[1:2])]
        for dx, dc in peers:
            got = stat[chip(dx) * C + core(dc), xs]
            parts.append((got[0:1], got[1:2]))
        peak = functools.reduce(jnp.maximum, [p for p, _ in parts])
        total = functools.reduce(jnp.add, [t * jnp.exp(p - peak) for p, t in parts])
        fac[z, i] = jnp.broadcast_to(factors[i] * jnp.exp(own[0:1] - peak) / total, (8, nb))
        if i == 0:
            evid = peak + jnp.log(total)
            mine = evid[:, 0:rows]
            for q in range(1, C):
                mine = jnp.where(c == q, evid[:, q * rows : (q + 1) * rows], mine)
            evid_ref[...] = mine
    for d in range(1, Z):
        remote(fac.at[z], fac.at[z], v_send.at[d - 1], v_recv.at[z], dev(zoff(d), x, c))

    def weights(zz):
        return jnp.concatenate(
            [(all_w[i, zz].astype(jnp.float32) * fac[zz, i, 0:1]).astype(jnp.bfloat16) for i in range(X)], axis=1
        )

    own_p = grid_buf[:, :, :, pl.ds(pl.multiple_of(z * pb, pb), pb)].reshape(X * nb, pb)
    with scope("prod0"):
        sums_ref[...] = jnp.dot(weights(z), own_p, preferred_element_type=jnp.float32)

    def second_step(src, right):
        for dx in range(1, X):
            with scope("psec"):
                arrive(p_block(src, dx, c), p_recv.at[src, dx, c])
        for cp in p_second(src):
            cp.start()

    def add_step(src, right):
        for i in range(X):
            w_wait(i)(src, right)
        with scope("vw"):
            arrive(fac.at[src], v_recv.at[src])
        with scope("addw"):
            for dx in range(X):
                for dc in range(1, C):
                    arrive(p_block(src, dx, core(dc)), p_recv.at[src, dx, core(dc)])
        with scope("addp"):
            sums_ref[...] += jnp.dot(weights(src), all_p[src].reshape(X * nb, pb), preferred_element_type=jnp.float32)

    @pl.loop(1, Z + 1)
    def _(d):
        @pl.when(d < Z)
        def _():
            for i in range(X - 1):
                @pl.when(d > early)
                def _():
                    sides(d, w_forward(i))
            sides(d, w_forward(X - 1))
            sides(d, second_step)

        @pl.when(d > 1)
        def _():
            sides(d - 1, add_step)

    with scope("drain"):
        for cp in started:
            cp.wait_send()
        for d in range(1, Z):
            p_copy(d).wait_send()

        def end_step(src, right):
            for cp in p_forward(src) + p_second(src):
                cp.wait_send()
            for i in range(X):
                @pl.when(forwards(src, right))
                def _():
                    for q in range(G):
                        w_go(i, src, q, right).wait_send()

        @pl.loop(1, Z)
        def _(d):
            sides(d, end_step)

        for i in range(X):
            for q in range(G):
                if Z > 2:
                    @pl.when(has_two)
                    def _():
                        w_two(i, q).wait_send()

                @pl.when(z < Z - 1)
                def _():
                    w_go(i, z, q, True).wait_send()

                @pl.when(z > 0)
                def _():
                    w_go(i, z, q, False).wait_send()


def exchange(mesh, images, templates, group_ids, group_ctf, group_prec, log_prior, class_mask):
    Z, X, C = mesh.shape["img"], mesh.shape["tpl"], mesh.shape["sub"]
    S = X * C
    rows, pix = images.shape
    refs = templates.shape[0]
    nb = C * rows
    pb = pix // Z
    H, G = PIECES, PARTS
    vmem = pl.BlockSpec(memory_space=pltpu.VMEM)
    anyw = pl.BlockSpec(memory_space=pl.ANY)
    dma = pltpu.SemaphoreType.DMA
    f32, bf16 = jnp.float32, jnp.bfloat16
    x1, c1, z1 = max(X - 1, 1), max(C - 1, 1), max(Z - 1, 1)
    class_sums, evid = pl.pallas_call(
        functools.partial(exchange_kernel, (Z, X, C, H, G)),
        out_shape=(
            pltpu.VMEM((refs, pb), f32),
            pltpu.VMEM((1, rows), f32),
        ),
        in_specs=[anyw] * 7,
        out_specs=(vmem, vmem),
        scratch_shapes=[
            pltpu.VMEM((X, 1, nb), jnp.int32),
            pltpu.SMEM(group_ctf.shape, f32),
            pltpu.SMEM(group_prec.shape, f32),
            pltpu.SMEM(log_prior.shape, f32),
            pltpu.SMEM(class_mask.shape, jnp.int32),
            pltpu.VMEM((X, C, rows, pix), bf16),
            pltpu.VMEM((refs, pix), bf16),
            pltpu.VMEM((refs, nb), f32),
            pltpu.VMEM((refs, nb), f32),
            pltpu.VMEM((refs, nb), f32),
            pltpu.VMEM((X, Z, refs, nb), bf16),
            pltpu.VMEM((Z, X, C, rows, pb), bf16),
            pltpu.VMEM((X, 8, nb), f32),
            pltpu.VMEM((S, X, 8, nb), f32),
            pltpu.VMEM((Z, X, 8, nb), f32),
            dma((5,)), dma(()), dma(()), dma((c1,)), dma((C,)), dma((x1, H)), dma((X, C, H)), dma((x1, H, c1)),
            dma((z1,)), dma((Z, X, C)), dma((Z, X, C)),
            dma((2, X, Z, G)), dma((X, G)), dma((X, Z, G)), dma((max(S - 1, 1),)), dma((S,)), dma((z1,)), dma((Z,)),
        ],
        compiler_params=pltpu.CompilerParams(
            collective_id=0, has_side_effects=True, vmem_limit_bytes=56 * 1024 * 1024
        ),
    )(group_ids.reshape(X, 1, nb), group_ctf, group_prec, log_prior, class_mask, images, templates)
    return class_sums, evid.reshape(rows)


def solution(mesh):
    placed = (
        P(("groups", "img", "tpl", "sub"), None),
        P(("groups", "tpl", "sub"), None),
        P(("groups", "img")),
        P("groups"),
        P("groups"),
        P("groups"),
        P("groups"),
    )
    return jax.shard_map(
        functools.partial(exchange, mesh),
        mesh=mesh,
        in_specs=placed,
        out_specs=(P(("groups", "tpl", "sub"), "img"), P(("groups", "img", "tpl", "sub"))),
        check_vma=False,
    )
```

time: 47.9 us -> 39.4 us (0.82)
  Pallas kernels: 45 us -> 36.4 us
    pallas_call x1, Pallas kernels: 45 us -> 36.4 us  [exchange(): pl.pallas_call(functools.partial(exchange_kernel, (Z, X, C, H, G)), out_s...]
where the time goes in v1:
time: 39.4 us; the launch traced here: 38.8 us
  Pallas kernels  36.4 us (92%)
  local copies, waits for them, and re-layouts  1.83 us (5%)
  between operations  0.64 us (2%)
    pallas_call x1, Pallas kernels, exchange(): pl.pallas_call(functools.partial(exchange_kernel, (Z, X, C, H, G)), out_s...  36.4 us
    unnamed x2, local copies, waits for them, and re-layouts  1.83 us

profile of v1, /device:TPU:0, one launch (start us, length us, event | category | flops | bytes accessed | tf_op | source)
XLA Modules:
  0.0 38.8 jit_solution(6363129274761135191)
XLA Ops:
  0.6 36.4 %shard_map.86 = (f32[512,1024]{1,0:T(8,128)S(1)}, f32[1,64]{1,0:T(1,128)S(1)}) custom-call(s32[2,1,128]{2,1,0:T(1,128)} %bitcast.3, f32[32]{0:T(128)} %ctf_in.1, f32[32]{0:T(128)} %prec_in.1, f32[128]{0:T(128)} %prior_in.1, s32[128]{0:T(128)} %mask_in.1, bf16[64,4096]{1,0:T(8,128)(2,1)} %images.1, bf16[512,4096]{1,0:T(8,128)(2,1)} %templates.1), custom_call_target="tpu_custom_call" | custom-call | tf_op jit(solution)/shard_map/pallas_call | solution.py:409
  37.0 1.3 %copy.11 = f32[512,1024]{1,0:T(8,128)} copy(f32[512,1024]{1,0:T(8,128)S(1)} %get-tuple-element.6) | data formatting | bytes 4194304
  38.3 0.5 %copy.12 = f32[64]{0:T(128)} copy(f32[64]{0:T(128)S(1)} %bitcast.2) | data formatting | bytes 512

commit v2 on v1

--- a/solution.py
+++ b/solution.py
@@ -9,7 +9,8 @@
 ROTS = 16
 MASKED = -1e30
 PIECES = 2
-PARTS = 2
+PARTS = 4
+NORM = 64
 MESH = pl.DeviceIdType.MESH
 
 
@@ -17,8 +18,7 @@
     sizes, ids_in, ctf_in, prec_in, prior_in, mask_in, images, templates,
     sums_ref, evid_ref,
     ids_ref, ctf_ref, prec_ref, prior_ref, mask_ref, grid_buf, tmpl, tnorm, base, act, all_w, all_p, own_stat, stat, fac,
-    in_sem, tmpl_sem, own_sem, c_send, c_recv, a_send, a_recv, f_send, p_send, p_recv, g_send,
-    w_send, w_far, w_recv, s_send, s_recv, v_send, v_recv,
+    in_sem, tmpl_sem, own_sem, sent, c_recv, a_recv, p_recv, w_recv, s_recv, v_recv, up,
 ):
     Z, X, C, H, G = sizes
     S = X * C
@@ -48,12 +48,15 @@
 
     peers = [(dx, dc) for dx in range(X) for dc in range(C) if dx or dc]
     inner = (z > 0) & (z < Z - 1)
+    early = min(2, Z - 1)
 
     barrier = pltpu.get_barrier_semaphore()
     for dx, dc in peers:
         pl.semaphore_signal(barrier, inc=1, device_id=dev(z, chip(dx), core(dc)), device_id_type=MESH)
-    for d in range(1, Z):
-        pl.semaphore_signal(barrier, inc=1, device_id=dev(zoff(d), x, c), device_id_type=MESH)
+
+    @pl.loop(z + 1, Z)
+    def _(zz):
+        pl.semaphore_signal(barrier, inc=1, device_id=dev(zz, x, c), device_id_type=MESH)
 
     started = []
 
@@ -85,17 +88,21 @@
     own_copy = local(images, grid_buf.at[0, c], own_sem)
 
     with scope("barrier"):
-        pl.semaphore_wait(barrier, S - 1 + Z - 1)
+        pl.semaphore_wait(barrier, S - 1 + z)
+
+    @pl.loop(0, z)
+    def _(zz):
+        pl.semaphore_signal(up.at[z], inc=1, device_id=dev(zz, x, c), device_id_type=MESH)
 
     def piece(i, cc, h):
         return grid_buf.at[i, cc, pl.ds(h * hr, hr), :]
 
     for dc in range(1, C):
-        remote(images, grid_buf.at[0, c], c_send.at[dc - 1], c_recv.at[c], dev(z, x, core(dc)))
+        remote(images, grid_buf.at[0, c], sent, c_recv.at[c], dev(z, x, core(dc)))
     for h in range(H):
         for dx in range(1, X):
             remote(
-                images.at[pl.ds(h * hr, hr), :], piece(X - dx, c, h), a_send.at[dx - 1, h], a_recv.at[X - dx, c, h],
+                images.at[pl.ds(h * hr, hr), :], piece(X - dx, c, h), sent, a_recv.at[X - dx, c, h],
                 dev(z, chip(dx), c),
             )
 
@@ -105,14 +112,26 @@
     def p_copy(d):
         zz = zoff(d)
         cols = pl.ds(pl.multiple_of(zz * pb, pb), pb)
-        return copy(images.at[:, cols], p_block(z, 0, c), p_send.at[d - 1], p_recv.at[z, 0, c], dev(zz, x, c))
+        return copy(images.at[:, cols], p_block(z, 0, c), sent, p_recv.at[z, 0, c], dev(zz, x, c))
 
     def outer(d):
         zz = zoff(d)
         return (zz == 0) | (zz == Z - 1)
 
+    def crosses(zz):
+        return (2 * z < Z) != (2 * zz < Z)
+
+    def p_send_inner(late):
+        for d in range(1, Z):
+            over = crosses(zoff(d)) & jnp.logical_not(inner)
+            first = (z == 0) & (zoff(d) == 1)
+
+            @pl.when(jnp.logical_not(outer(d) | first) & (over if late else jnp.logical_not(over)))
+            def _():
+                p_copy(d).start()
+
     for d in range(1, Z):
-        @pl.when(outer(d))
+        @pl.when(zoff(d) == 0)
         def _():
             p_copy(d).start()
 
@@ -141,11 +160,32 @@
         tmpl_copy.wait()
 
     with scope("tnorm"):
-        @pl.loop(0, refs // 16)
+        @pl.loop(0, refs // NORM)
         def _(i):
-            rws = pl.ds(pl.multiple_of(i * 16, 16), 16)
+            rws = pl.ds(pl.multiple_of(i * NORM, NORM), NORM)
             t = tmpl[rws, :].astype(jnp.float32)
-            tnorm[rws, :] = jnp.broadcast_to(jnp.sum(t * t, axis=1, keepdims=True), (16, nb))
+            tnorm[rws, :] = jnp.broadcast_to(jnp.sum(t * t, axis=1, keepdims=True), (NORM, nb))
+
+    def p_far(first):
+        @pl.loop(first, Z)
+        def _(zz):
+            pl.semaphore_wait(up.at[zz], 1)
+
+        for d in range(1, Z):
+            @pl.when(zoff(d) == Z - 1)
+            def _():
+                p_copy(d).start()
+
+    with scope("up"):
+        if Z > 2:
+            @pl.when(z == 0)
+            def _():
+                pl.semaphore_wait(up.at[1], 1)
+                p_copy(1).start()
+
+            @pl.when(z > 0)
+            def _():
+                p_far(z + 1)
 
     def w_part(i, zz, q):
         return all_w.at[i, zz, pl.ds(q * gr, gr), :]
@@ -153,13 +193,13 @@
     def w_go(i, zz, q, right):
         step = 1 if right else -1
         return copy(
-            w_part(i, zz, q), w_part(i, zz, q), w_send.at[0 if right else 1, i, zz, q], w_recv.at[i, zz, q],
+            w_part(i, zz, q), w_part(i, zz, q), sent, w_recv.at[i, zz, q],
             dev(lax.rem(z + step + Z, Z), x, c),
         )
 
     def w_two(i, q):
         zz = lax.rem(jnp.where(z == 0, z + 2, z - 2) + Z, Z)
-        return copy(w_part(i, z, q), w_part(i, z, q), w_far.at[i, q], w_recv.at[i, z, q], dev(zz, x, c))
+        return copy(w_part(i, z, q), w_part(i, z, q), sent, w_recv.at[i, z, q], dev(zz, x, c))
 
     has_two = ((z == 0) | (z == Z - 1)) if Z > 2 else None
 
@@ -177,28 +217,33 @@
         def _():
             fn(z + d, False)
 
-    def w_forward(i):
+    def w_forward(i, q):
         def fn(src, right):
             @pl.when(forwards(src, right))
             def _():
-                for q in range(G):
-                    with scope(f"wf{i}"):
-                        arrive(w_part(i, src, q), w_recv.at[i, src, q])
-                    w_go(i, src, q, right).start()
+                with scope(f"wf{i}"):
+                    arrive(w_part(i, src, q), w_recv.at[i, src, q])
+                w_go(i, src, q, right).start()
         return fn
 
-    def w_wait(i):
+    def w_forwards(i, d, side, parts=range(G)):
+        def fn(src, right):
+            if side is None or side == right:
+                for q in parts:
+                    w_forward(i, q)(src, right)
+        sides(d, fn)
+
+    def w_wait(i, q):
         def fn(src, right):
             @pl.when(jnp.logical_not(forwards(src, right)))
             def _():
-                for q in range(G):
-                    with scope(f"ww{i}"):
-                        arrive(w_part(i, src, q), w_recv.at[i, src, q])
+                with scope(f"ww{i}"):
+                    arrive(w_part(i, src, q), w_recv.at[i, src, q])
         return fn
 
     def scores(i):
         pixels = grid_buf[i].reshape(nb, pix)
-        raw = lax.dot_general(tmpl[...], pixels, (((1,), (1,)), ((), ())), preferred_element_type=jnp.float32)
+        raw = lax.dot_general(pixels, tmpl[...], (((1,), (1,)), ((), ())), preferred_element_type=jnp.float32).T
         live = act[...] > 0.0
         values = jnp.where(live, factors[i] * raw - penalties[i] * tnorm[...] + base[...], MASKED)
         peak = jnp.max(values, axis=0, keepdims=True)
@@ -207,6 +252,8 @@
         total = jnp.sum(terms, axis=0, keepdims=True)
         row = lax.broadcasted_iota(jnp.int32, (8, nb), 0)
         own_stat[chip(i)] = jnp.where(row == 0, peak, total)
+
+    def w_start(i):
         for q in range(G):
             if Z > 2:
                 @pl.when(has_two)
@@ -224,16 +271,16 @@
     def p_forward(zz):
         out = []
         for dx in range(1, X):
-            out.append(copy(p_block(zz, 0, c), p_block(zz, X - dx, c), g_send.at[zz, dx - 1, 0], p_recv.at[zz, X - dx, c], dev(z, chip(dx), c)))
+            out.append(copy(p_block(zz, 0, c), p_block(zz, X - dx, c), sent, p_recv.at[zz, X - dx, c], dev(z, chip(dx), c)))
         for dc in range(1, C):
-            out.append(copy(p_block(zz, 0, c), p_block(zz, 0, c), g_send.at[zz, X - 1, dc - 1], p_recv.at[zz, 0, c], dev(z, x, core(dc))))
+            out.append(copy(p_block(zz, 0, c), p_block(zz, 0, c), sent, p_recv.at[zz, 0, c], dev(z, x, core(dc))))
         return out
 
     def p_second(zz):
         out = []
         for dx in range(1, X):
             for dc in range(1, C):
-                out.append(copy(p_block(zz, dx, c), p_block(zz, dx, c), g_send.at[zz, dx - 1, dc], p_recv.at[zz, dx, c], dev(z, x, core(dc))))
+                out.append(copy(p_block(zz, dx, c), p_block(zz, dx, c), sent, p_recv.at[zz, dx, c], dev(z, x, core(dc))))
         return out
 
     def p_start(zz, right):
@@ -242,11 +289,20 @@
         for cp in p_forward(zz):
             cp.start()
 
+    def p_slot(d, n):
+        def fn(src, right):
+            slot = jnp.where(inner & crosses(src), 2, jnp.where(inner | (d == 1), 0, 1))
+
+            @pl.when(slot == n)
+            def _():
+                p_start(src, right)
+        sides(d, fn)
+
     def gather(dx, h):
         with scope(f"gath{h}"):
             arrive(piece(dx, c, h), a_recv.at[dx, c, h])
         for dc in range(1, C):
-            remote(piece(dx, c, h), piece(dx, c, h), f_send.at[dx - 1, h, dc - 1], a_recv.at[dx, c, h], dev(z, x, core(dc)))
+            remote(piece(dx, c, h), piece(dx, c, h), sent, a_recv.at[dx, c, h], dev(z, x, core(dc)))
 
     own_copy.wait()
     with scope("own"):
@@ -254,39 +310,40 @@
             arrive(grid_buf.at[0, core(dc)], c_recv.at[core(dc)])
     with scope("sc0"):
         scores(0)
-    for d in range(1, Z):
-        @pl.when(jnp.logical_not(outer(d)))
-        def _():
-            p_copy(d).start()
-
-    early = min(2, Z - 1)
+
+    @pl.when(z == 0)
+    def _():
+        p_far(min(2, Z - 1))
+
+    w_start(0)
+    p_send_inner(False)
+
     for dx in range(1, X):
         for h in range(H):
             gather(dx, h)
-            if dx == 1 and h == 0:
-                sides(1, w_forward(0))
-
-                @pl.when(jnp.logical_not(inner))
-                def _():
-                    for d in range(1, early + 1):
-                        sides(d, p_start)
+            if h == H - 2:
+                for d in range(early, 1, -1):
+                    w_forwards(dx - 1, d, False)
+                w_forwards(dx - 1, 1, False, range(G // 2))
             elif h == H - 1:
-                for d in range(2 if dx == 1 else 1, early + 1):
-                    sides(d, w_forward(dx - 1))
+                w_forwards(dx - 1, 1, False, range(G // 2, G))
+        if dx == X - 1:
+            p_send_inner(True)
+            for d in range(1, early + 1):
+                p_slot(d, 0)
         with scope(f"arrA{dx}"):
             for h in range(H):
                 for dc in range(1, C):
                     arrive(piece(dx, core(dc), h), a_recv.at[dx, core(dc), h])
         with scope(f"sc{dx}"):
             scores(dx)
+        w_start(dx)
 
     for i, (dx, dc) in enumerate(peers):
-        remote(own_stat, stat.at[s], s_send.at[i], s_recv.at[s], dev(z, chip(dx), core(dc)))
-
-    @pl.when(inner)
-    def _():
-        for d in range(1, early + 1):
-            sides(d, p_start)
+        remote(own_stat, stat.at[s], sent, s_recv.at[s], dev(z, chip(dx), core(dc)))
+
+    for d in range(1, early + 1):
+        p_slot(d, 1)
 
     @pl.loop(early + 1, Z)
     def _(d):
@@ -313,16 +370,16 @@
                 mine = jnp.where(c == q, evid[:, q * rows : (q + 1) * rows], mine)
             evid_ref[...] = mine
     for d in range(1, Z):
-        remote(fac.at[z], fac.at[z], v_send.at[d - 1], v_recv.at[z], dev(zoff(d), x, c))
-
-    def weights(zz):
+        remote(fac.at[z], fac.at[z], sent, v_recv.at[z], dev(zoff(d), x, c))
+
+    def weights(zz, chunks, rws):
         return jnp.concatenate(
-            [(all_w[i, zz].astype(jnp.float32) * fac[zz, i, 0:1]).astype(jnp.bfloat16) for i in range(X)], axis=1
+            [(all_w[i, zz, rws, :].astype(jnp.float32) * fac[zz, i, 0:1]).astype(jnp.bfloat16) for i in chunks], axis=1
         )
 
-    own_p = grid_buf[:, :, :, pl.ds(pl.multiple_of(z * pb, pb), pb)].reshape(X * nb, pb)
-    with scope("prod0"):
-        sums_ref[...] = jnp.dot(weights(z), own_p, preferred_element_type=jnp.float32)
+    def product(zz, chunks, rws):
+        block = all_p[zz, chunks[0] : chunks[-1] + 1].reshape(len(chunks) * nb, pb)
+        sums_ref[rws, :] += jnp.dot(weights(zz, chunks, rws), block, preferred_element_type=jnp.float32)
 
     def second_step(src, right):
         for dx in range(1, X):
@@ -331,32 +388,64 @@
         for cp in p_second(src):
             cp.start()
 
-    def add_step(src, right):
+    def add_step(chunks):
+        def fn(src, right):
+            for i in chunks:
+                for q in range(G):
+                    w_wait(i, q)(src, right)
+            with scope("vw"):
+                arrive(fac.at[src], v_recv.at[src])
+            with scope("addw"):
+                for dx in range(X):
+                    for dc in range(1, C):
+                        arrive(p_block(src, dx, core(dc)), p_recv.at[src, dx, core(dc)])
+            with scope("addp"):
+                product(src, chunks, pl.ds(0, refs))
+        return fn
+
+    def last_step(q):
+        def fn(src, right):
+            w_wait(X - 1, q)(src, right)
+            with scope(f"last{q}"):
+                product(src, range(X - 1, X), pl.ds(q * gr, gr))
+        return fn
+
+    for i in range(X - 1):
+        for d in range(early, 0, -1):
+            w_forwards(i, d, True)
+    for d in range(early, 0, -1):
+        p_slot(d, 2)
+        if d > 1:
+            w_forwards(X - 1, d, None)
+    w_forwards(X - 1, 1, None)
+
+    @pl.loop(early + 1, Z)
+    def _(d):
         for i in range(X):
-            w_wait(i)(src, right)
-        with scope("vw"):
-            arrive(fac.at[src], v_recv.at[src])
-        with scope("addw"):
-            for dx in range(X):
-                for dc in range(1, C):
-                    arrive(p_block(src, dx, core(dc)), p_recv.at[src, dx, core(dc)])
-        with scope("addp"):
-            sums_ref[...] += jnp.dot(weights(src), all_p[src].reshape(X * nb, pb), preferred_element_type=jnp.float32)
-
-    @pl.loop(1, Z + 1)
+            w_forwards(i, d, None)
+
+    own_p = grid_buf[:, :, :, pl.ds(pl.multiple_of(z * pb, pb), pb)].reshape(X * nb, pb)
+    with scope("prod0"):
+        sums_ref[...] = jnp.dot(weights(z, range(X), pl.ds(0, refs)), own_p, preferred_element_type=jnp.float32)
+
+    for d in range(1, early + 1):
+        sides(d, second_step)
+
+    @pl.loop(early + 1, Z)
     def _(d):
-        @pl.when(d < Z)
-        def _():
-            for i in range(X - 1):
-                @pl.when(d > early)
-                def _():
-                    sides(d, w_forward(i))
-            sides(d, w_forward(X - 1))
-            sides(d, second_step)
-
-        @pl.when(d > 1)
-        def _():
-            sides(d - 1, add_step)
+        sides(d, second_step)
+
+    sides(1, add_step(range(X)))
+
+    @pl.loop(2, Z)
+    def _(d):
+        sides(d, add_step(range(max(X - 1, 1))))
+
+    if X > 1:
+        @pl.loop(0, Z - 2)
+        def _(d):
+            for q in range(G):
+                sides(Z - 1 - d, last_step(q))
 
     with scope("drain"):
         for cp in started:
@@ -405,7 +494,6 @@
     anyw = pl.BlockSpec(memory_space=pl.ANY)
     dma = pltpu.SemaphoreType.DMA
     f32, bf16 = jnp.float32, jnp.bfloat16
-    x1, c1, z1 = max(X - 1, 1), max(C - 1, 1), max(Z - 1, 1)
     class_sums, evid = pl.pallas_call(
         functools.partial(exchange_kernel, (Z, X, C, H, G)),
         out_shape=(
@@ -430,9 +518,8 @@
             pltpu.VMEM((X, 8, nb), f32),
             pltpu.VMEM((S, X, 8, nb), f32),
             pltpu.VMEM((Z, X, 8, nb), f32),
-            dma((5,)), dma(()), dma(()), dma((c1,)), dma((C,)), dma((x1, H)), dma((X, C, H)), dma((x1, H, c1)),
-            dma((z1,)), dma((Z, X, C)), dma((Z, X, C)),
-            dma((2, X, Z, G)), dma((X, G)), dma((X, Z, G)), dma((max(S - 1, 1),)), dma((S,)), dma((z1,)), dma((Z,)),
+            dma((5,)), dma(()), dma(()), dma(()), dma((C,)), dma((X, C, H)), dma((Z, X, C)), dma((X, Z, G)), dma((S,)), dma((Z,)),
+            pltpu.SemaphoreType.REGULAR((Z,)),
         ],
         compiler_params=pltpu.CompilerParams(
             collective_id=0, has_side_effects=True, vmem_limit_bytes=56 * 1024 * 1024

time: 39.4 us -> 38.2 us (0.970)
  the two profiles are of different devices: /device:TPU:0 before, /device:TPU:24 now
where the time goes in v2:
time: 38.2 us; the launch traced here: 38.1 us
  Pallas kernels  35.6 us (93%)
  local copies, waits for them, and re-layouts  1.83 us (5%)
  between operations  0.64 us (2%)
    pallas_call x1, Pallas kernels, exchange(): pl.pallas_call(functools.partial(exchange_kernel, (Z, X, C, H, G)), out_s...  35.6 us
    unnamed x2, local copies, waits for them, and re-layouts  1.83 us

profile of v2, /device:TPU:24, one launch (start us, length us, event | category | flops | bytes accessed | tf_op | source)
XLA Modules:
  0.0 38.1 jit_solution(2306142486407315184)
XLA Ops:
  0.6 35.6 %shard_map.86 = (f32[512,1024]{1,0:T(8,128)S(1)}, f32[1,64]{1,0:T(1,128)S(1)}) custom-call(s32[2,1,128]{2,1,0:T(1,128)} %bitcast.3, f32[32]{0:T(128)} %ctf_in.1, f32[32]{0:T(128)} %prec_in.1, f32[128]{0:T(128)} %prior_in.1, s32[128]{0:T(128)} %mask_in.1, bf16[64,4096]{1,0:T(8,128)(2,1)} %images.1, bf16[512,4096]{1,0:T(8,128)(2,1)} %templates.1), custom_call_target="tpu_custom_call" | custom-call | tf_op jit(solution)/shard_map/pallas_call | solution.py:497
  36.2 1.3 %copy.11 = f32[512,1024]{1,0:T(8,128)} copy(f32[512,1024]{1,0:T(8,128)S(1)} %get-tuple-element.6) | data formatting | bytes 4194304
  37.5 0.5 %copy.12 = f32[64]{0:T(128)} copy(f32[64]{0:T(128)S(1)} %bitcast.2) | data formatting | bytes 512

commit v3 on v2

--- a/solution.py
+++ b/solution.py
@@ -11,6 +11,7 @@
 PIECES = 2
 PARTS = 4
 NORM = 64
+FLUSH = 4
 MESH = pl.DeviceIdType.MESH
 
 
@@ -102,7 +103,7 @@
     for h in range(H):
         for dx in range(1, X):
             remote(
-                images.at[pl.ds(h * hr, hr), :], piece(X - dx, c, h), sent, a_recv.at[X - dx, c, h],
+                images.at[pl.ds(h * hr, hr), :], piece(X - dx, c, h), sent, a_recv.at[X - dx, h],
                 dev(z, chip(dx), c),
             )
 
@@ -112,7 +113,7 @@
     def p_copy(d):
         zz = zoff(d)
         cols = pl.ds(pl.multiple_of(zz * pb, pb), pb)
-        return copy(images.at[:, cols], p_block(z, 0, c), sent, p_recv.at[z, 0, c], dev(zz, x, c))
+        return copy(images.at[:, cols], p_block(z, 0, c), sent, p_recv.at[z, 0], dev(zz, x, c))
 
     def outer(d):
         zz = zoff(d)
@@ -121,12 +122,13 @@
     def crosses(zz):
         return (2 * z < Z) != (2 * zz < Z)
 
-    def p_send_inner(late):
+    def p_send_inner(n):
         for d in range(1, Z):
             over = crosses(zoff(d)) & jnp.logical_not(inner)
             first = (z == 0) & (zoff(d) == 1)
-
-            @pl.when(jnp.logical_not(outer(d) | first) & (over if late else jnp.logical_not(over)))
+            slot = jnp.where(over, jnp.where(z == 0, 2, 1), 0)
+
+            @pl.when(jnp.logical_not(outer(d) | first) & (slot == n))
             def _():
                 p_copy(d).start()
 
@@ -190,16 +192,16 @@
     def w_part(i, zz, q):
         return all_w.at[i, zz, pl.ds(q * gr, gr), :]
 
+    def w_sem(i, src, dst, q):
+        return w_recv.at[i, lax.rem(src - dst + Z - 1, Z), q]
+
     def w_go(i, zz, q, right):
-        step = 1 if right else -1
-        return copy(
-            w_part(i, zz, q), w_part(i, zz, q), sent, w_recv.at[i, zz, q],
-            dev(lax.rem(z + step + Z, Z), x, c),
-        )
+        to = lax.rem(z + (1 if right else -1) + Z, Z)
+        return copy(w_part(i, zz, q), w_part(i, zz, q), sent, w_sem(i, zz, to, q), dev(to, x, c))
 
     def w_two(i, q):
         zz = lax.rem(jnp.where(z == 0, z + 2, z - 2) + Z, Z)
-        return copy(w_part(i, z, q), w_part(i, z, q), sent, w_recv.at[i, z, q], dev(zz, x, c))
+        return copy(w_part(i, z, q), w_part(i, z, q), sent, w_sem(i, z, zz, q), dev(zz, x, c))
 
     has_two = ((z == 0) | (z == Z - 1)) if Z > 2 else None
 
@@ -222,7 +224,7 @@
             @pl.when(forwards(src, right))
             def _():
                 with scope(f"wf{i}"):
-                    arrive(w_part(i, src, q), w_recv.at[i, src, q])
+                    arrive(w_part(i, src, q), w_sem(i, src, z, q))
                 w_go(i, src, q, right).start()
         return fn
 
@@ -238,7 +240,7 @@
             @pl.when(jnp.logical_not(forwards(src, right)))
             def _():
                 with scope(f"ww{i}"):
-                    arrive(w_part(i, src, q), w_recv.at[i, src, q])
+                    arrive(w_part(i, src, q), w_sem(i, src, z, q))
         return fn
 
     def scores(i):
@@ -254,12 +256,16 @@
         own_stat[chip(i)] = jnp.where(row == 0, peak, total)
 
     def w_start(i):
+        if i == X - 1:
+            p_send_inner(2)
+
+        if Z > 2:
+            @pl.when(has_two)
+            def _():
+                for q in range(G):
+                    w_two(i, q).start()
+
         for q in range(G):
-            if Z > 2:
-                @pl.when(has_two)
-                def _():
-                    w_two(i, q).start()
-
             @pl.when(z < Z - 1)
             def _():
                 w_go(i, z, q, True).start()
@@ -271,27 +277,28 @@
     def p_forward(zz):
         out = []
         for dx in range(1, X):
-            out.append(copy(p_block(zz, 0, c), p_block(zz, X - dx, c), sent, p_recv.at[zz, X - dx, c], dev(z, chip(dx), c)))
+            out.append(copy(p_block(zz, 0, c), p_block(zz, X - dx, c), sent, p_recv.at[zz, X - dx], dev(z, chip(dx), c)))
         for dc in range(1, C):
-            out.append(copy(p_block(zz, 0, c), p_block(zz, 0, c), sent, p_recv.at[zz, 0, c], dev(z, x, core(dc))))
+            out.append(copy(p_block(zz, 0, c), p_block(zz, 0, c), sent, p_recv.at[zz, X + C - 1 - dc], dev(z, x, core(dc))))
         return out
 
     def p_second(zz):
         out = []
         for dx in range(1, X):
             for dc in range(1, C):
-                out.append(copy(p_block(zz, dx, c), p_block(zz, dx, c), sent, p_recv.at[zz, dx, c], dev(z, x, core(dc))))
+                out.append(copy(p_block(zz, dx, c), p_block(zz, dx, c), sent, p_recv.at[zz, X + C - 1 - dc], dev(z, x, core(dc))))
         return out
 
     def p_start(zz, right):
         with scope("pst"):
-            arrive(p_block(zz, 0, c), p_recv.at[zz, 0, c])
+            arrive(p_block(zz, 0, c), p_recv.at[zz, 0])
         for cp in p_forward(zz):
             cp.start()
 
     def p_slot(d, n):
         def fn(src, right):
-            slot = jnp.where(inner & crosses(src), 2, jnp.where(inner | (d == 1), 0, 1))
+            far = 3 if d == 1 else 2
+            slot = jnp.where(inner & crosses(src), far, jnp.where(inner | (d == 1), 0, 1))
 
             @pl.when(slot == n)
             def _():
@@ -300,9 +307,9 @@
 
     def gather(dx, h):
         with scope(f"gath{h}"):
-            arrive(piece(dx, c, h), a_recv.at[dx, c, h])
+            arrive(piece(dx, c, h), a_recv.at[dx, h])
         for dc in range(1, C):
-            remote(piece(dx, c, h), piece(dx, c, h), sent, a_recv.at[dx, c, h], dev(z, x, core(dc)))
+            remote(piece(dx, c, h), piece(dx, c, h), sent, a_recv.at[dx, H + C - 1 - dc], dev(z, x, core(dc)))
 
     own_copy.wait()
     with scope("own"):
@@ -316,7 +323,9 @@
         p_far(min(2, Z - 1))
 
     w_start(0)
-    p_send_inner(False)
+    if X == 1:
+        p_send_inner(1)
+    p_send_inner(0)
 
     for dx in range(1, X):
         for h in range(H):
@@ -324,24 +333,28 @@
             if h == H - 2:
                 for d in range(early, 1, -1):
                     w_forwards(dx - 1, d, False)
+                    w_forwards(dx - 1, d, True, range(G - 1))
                 w_forwards(dx - 1, 1, False, range(G // 2))
             elif h == H - 1:
+                for d in range(early, 1, -1):
+                    w_forwards(dx - 1, d, True, range(G - 1, G))
                 w_forwards(dx - 1, 1, False, range(G // 2, G))
         if dx == X - 1:
-            p_send_inner(True)
+            p_send_inner(1)
             for d in range(1, early + 1):
                 p_slot(d, 0)
         with scope(f"arrA{dx}"):
-            for h in range(H):
-                for dc in range(1, C):
-                    arrive(piece(dx, core(dc), h), a_recv.at[dx, core(dc), h])
+            for dc in range(1, C):
+                arrive(grid_buf.at[dx, core(dc)], a_recv.at[dx, H + dc - 1])
         with scope(f"sc{dx}"):
             scores(dx)
         w_start(dx)
 
-    for i, (dx, dc) in enumerate(peers):
-        remote(own_stat, stat.at[s], sent, s_recv.at[s], dev(z, chip(dx), core(dc)))
-
+    for dx, dc in peers:
+        remote(own_stat, stat.at[s], sent, s_recv, dev(z, chip(dx), core(dc)))
+
+    for i in range(X - 1):
+        w_forwards(i, 1, True)
     for d in range(1, early + 1):
         p_slot(d, 1)
 
@@ -350,9 +363,7 @@
         sides(d, p_start)
 
     with scope("stat"):
-        for dx, dc in peers:
-            slot = chip(dx) * C + core(dc)
-            arrive(stat.at[slot], s_recv.at[slot])
+        arrive(stat.at[pl.ds(0, S - 1)], s_recv)
     for i in range(X):
         xs = chip(i)
         own = own_stat[xs]
@@ -384,7 +395,7 @@
     def second_step(src, right):
         for dx in range(1, X):
             with scope("psec"):
-                arrive(p_block(src, dx, c), p_recv.at[src, dx, c])
+                arrive(p_block(src, dx, c), p_recv.at[src, dx])
         for cp in p_second(src):
             cp.start()
 
@@ -396,9 +407,8 @@
             with scope("vw"):
                 arrive(fac.at[src], v_recv.at[src])
             with scope("addw"):
-                for dx in range(X):
-                    for dc in range(1, C):
-                        arrive(p_block(src, dx, core(dc)), p_recv.at[src, dx, core(dc)])
+                for dc in range(1, C):
+                    arrive(all_p.at[src, :, core(dc)], p_recv.at[src, X + dc - 1])
             with scope("addp"):
                 product(src, chunks, pl.ds(0, refs))
         return fn
@@ -410,13 +420,14 @@
                 product(src, range(X - 1, X), pl.ds(q * gr, gr))
         return fn
 
-    for i in range(X - 1):
-        for d in range(early, 0, -1):
-            w_forwards(i, d, True)
-    for d in range(early, 0, -1):
+    own_p = grid_buf[:, :, :, pl.ds(pl.multiple_of(z * pb, pb), pb)].reshape(X * nb, pb)
+    with scope("prod0"):
+        sums_ref[...] = jnp.dot(weights(z, range(X), pl.ds(0, refs)), own_p, preferred_element_type=jnp.float32)
+
+    for d in range(early, 1, -1):
         p_slot(d, 2)
-        if d > 1:
-            w_forwards(X - 1, d, None)
+        w_forwards(X - 1, d, None)
+    p_slot(1, 3)
     w_forwards(X - 1, 1, None)
 
     @pl.loop(early + 1, Z)
@@ -424,28 +435,46 @@
         for i in range(X):
             w_forwards(i, d, None)
 
-    own_p = grid_buf[:, :, :, pl.ds(pl.multiple_of(z * pb, pb), pb)].reshape(X * nb, pb)
-    with scope("prod0"):
-        sums_ref[...] = jnp.dot(weights(z, range(X), pl.ds(0, refs)), own_p, preferred_element_type=jnp.float32)
-
-    for d in range(1, early + 1):
-        sides(d, second_step)
-
-    @pl.loop(early + 1, Z)
+    def near(fn, over):
+        def at(src, right):
+            ok = crosses(src) if over else jnp.logical_not(crosses(src))
+
+            @pl.when(ok)
+            def _():
+                fn(src, right)
+        sides(1, at)
+
+    def lasts(d):
+        for q in range(G):
+            sides(d, last_step(q))
+
+    near(second_step, False)
+
+    @pl.loop(2, Z)
     def _(d):
         sides(d, second_step)
 
-    sides(1, add_step(range(X)))
-
-    @pl.loop(2, Z)
-    def _(d):
-        sides(d, add_step(range(max(X - 1, 1))))
-
-    if X > 1:
+    near(add_step(range(X)), False)
+    near(second_step, True)
+
+    @pl.when(inner)
+    def _():
+        @pl.loop(2, Z)
+        def _(d):
+            sides(d, add_step(range(X)))
+
+        near(add_step(range(X)), True)
+
+    @pl.when(jnp.logical_not(inner))
+    def _():
         @pl.loop(0, Z - 2)
-        def _(d):
-            for q in range(G):
-                sides(Z - 1 - d, last_step(q))
+        def _(e):
+            sides(Z - 1 - e, add_step(range(max(X - 1, 1))))
+            if X > 1:
+                lasts(Z - 1 - e)
+
+        if Z == 2:
+            near(add_step(range(X)), True)
 
     with scope("drain"):
         for cp in started:
@@ -480,6 +509,19 @@
                 @pl.when(z > 0)
                 def _():
                     w_go(i, z, q, False).wait_send()
+
+
+def flush_kernel(sums, evid, sums_out, evid_out, sem):
+    n = sem.shape[0] - 1
+    step = sums.shape[0] // n
+    copies = [pltpu.make_async_copy(evid, evid_out, sem.at[n])]
+    for i in range(n):
+        part = pl.ds(i * step, step)
+        copies.append(pltpu.make_async_copy(sums.at[part, :], sums_out.at[part, :], sem.at[i]))
+    for cp in copies:
+        cp.start()
+    for cp in copies:
+        cp.wait()
 
 
 def exchange(mesh, images, templates, group_ids, group_ctf, group_prec, log_prior, class_mask):
@@ -518,13 +560,21 @@
             pltpu.VMEM((X, 8, nb), f32),
             pltpu.VMEM((S, X, 8, nb), f32),
             pltpu.VMEM((Z, X, 8, nb), f32),
-            dma((5,)), dma(()), dma(()), dma(()), dma((C,)), dma((X, C, H)), dma((Z, X, C)), dma((X, Z, G)), dma((S,)), dma((Z,)),
+            dma((5,)), dma(()), dma(()), dma(()), dma((C,)), dma((X, H + C - 1)), dma((Z, X + C - 1)), dma((X, max(Z - 1, 1), G)), dma(()), dma((Z,)),
             pltpu.SemaphoreType.REGULAR((Z,)),
         ],
         compiler_params=pltpu.CompilerParams(
             collective_id=0, has_side_effects=True, vmem_limit_bytes=56 * 1024 * 1024
         ),
     )(group_ids.reshape(X, 1, nb), group_ctf, group_prec, log_prior, class_mask, images, templates)
+    class_sums, evid = pl.pallas_call(
+        flush_kernel,
+        out_shape=(jax.ShapeDtypeStruct((refs, pb), f32), jax.ShapeDtypeStruct((1, rows), f32)),
+        in_specs=[vmem, vmem],
+        out_specs=(anyw, anyw),
+        scratch_shapes=[dma((FLUSH + 1,))],
+        compiler_params=pltpu.CompilerParams(vmem_limit_bytes=1024 * 1024),
+    )(class_sums, evid)
     return class_sums, evid.reshape(rows)
 
 

time: 38.2 us -> 35.3 us (0.924)
  the two profiles are of different devices: /device:TPU:24 before, /device:TPU:0 now
where the time goes in v3:
time: 35.3 us; the launch traced here: 35.2 us
  Pallas kernels  34.5 us (98%)
  between operations  0.64 us (2%)
    pallas_call x1, Pallas kernels, exchange(): pl.pallas_call(functools.partial(exchange_kernel, (Z, X, C, H, G)), out_s...  33.2 us
    pallas_call x1, Pallas kernels, exchange(): pl.pallas_call(flush_kernel, out_shape=(jax.ShapeDtypeStruct((refs, pb),...  1.36 us

profile of v3, /device:TPU:0, one launch (start us, length us, event | category | flops | bytes accessed | tf_op | source)
XLA Modules:
  0.0 35.2 jit_solution(8009341543632403255)
XLA Ops:
  0.6 33.2 %shard_map.86 = (f32[512,1024]{1,0:T(8,128)S(1)}, f32[1,64]{1,0:T(1,128)S(1)}) custom-call(s32[2,1,128]{2,1,0:T(1,128)} %bitcast.2, f32[32]{0:T(128)} %ctf_in.1, f32[32]{0:T(128)} %prec_in.1, f32[128]{0:T(128)} %prior_in.1, s32[128]{0:T(128)} %mask_in.1, bf16[64,4096]{1,0:T(8,128)(2,1)} %images.1, bf16[512,4096]{1,0:T(8,128)(2,1)} %templates.1), custom_call_target="tpu_custom_call" | custom-call | tf_op jit(solution)/shard_map/pallas_call | solution.py:539
  33.8 1.4 %shard_map.87 = (f32[512,1024]{1,0:T(8,128)}, f32[1,64]{1,0:T(1,128)}) custom-call(f32[512,1024]{1,0:T(8,128)S(1)} %get-tuple-element.6.sums, f32[1,64]{1,0:T(1,128)S(1)} %get-tuple-element.7.evid), custom_call_target="tpu_custom_call" | custom-call | tf_op jit(solution)/shard_map/pallas_call | solution.py:570

commit v4 on v3

--- a/solution.py
+++ b/solution.py
@@ -8,7 +8,7 @@
 
 ROTS = 16
 MASKED = -1e30
-PIECES = 2
+PIECES = 4
 PARTS = 4
 NORM = 64
 FLUSH = 4
@@ -19,7 +19,7 @@
     sizes, ids_in, ctf_in, prec_in, prior_in, mask_in, images, templates,
     sums_ref, evid_ref,
     ids_ref, ctf_ref, prec_ref, prior_ref, mask_ref, grid_buf, tmpl, tnorm, base, act, all_w, all_p, own_stat, stat, fac,
-    in_sem, tmpl_sem, own_sem, sent, c_recv, a_recv, p_recv, w_recv, s_recv, v_recv, up,
+    in_sem, tmpl_sem, own_sem, sent, c_recv, a_recv, p_recv, w_recv, s_recv, v_recv, up, side,
 ):
     Z, X, C, H, G = sizes
     S = X * C
@@ -52,8 +52,13 @@
     early = min(2, Z - 1)
 
     barrier = pltpu.get_barrier_semaphore()
-    for dx, dc in peers:
-        pl.semaphore_signal(barrier, inc=1, device_id=dev(z, chip(dx), core(dc)), device_id_type=MESH)
+    for dc in range(1, C):
+        pl.semaphore_signal(barrier, inc=1, device_id=dev(z, x, core(dc)), device_id_type=MESH)
+
+    @pl.loop(x + 1, X)
+    def _(xx):
+        for cc in range(C):
+            pl.semaphore_signal(barrier, inc=1, device_id=dev(z, xx, cc), device_id_type=MESH)
 
     @pl.loop(z + 1, Z)
     def _(zz):
@@ -89,7 +94,12 @@
     own_copy = local(images, grid_buf.at[0, c], own_sem)
 
     with scope("barrier"):
-        pl.semaphore_wait(barrier, S - 1 + z)
+        pl.semaphore_wait(barrier, C - 1 + x * C + z)
+
+    @pl.loop(0, x)
+    def _(xx):
+        for cc in range(C):
+            pl.semaphore_signal(side, inc=1, device_id=dev(z, xx, cc), device_id_type=MESH)
 
     @pl.loop(0, z)
     def _(zz):
@@ -100,6 +110,40 @@
 
     for dc in range(1, C):
         remote(images, grid_buf.at[0, c], sent, c_recv.at[c], dev(z, x, core(dc)))
+    def p_block(zz, i, cc):
+        return all_p.at[zz, i, cc]
+
+    def p_copy(d):
+        zz = zoff(d)
+        cols = pl.ds(pl.multiple_of(zz * pb, pb), pb)
+        return copy(images.at[:, cols], p_block(z, 0, c), sent, p_recv.at[z, 0], dev(zz, x, c))
+
+    def outer(d):
+        zz = zoff(d)
+        return (zz == 0) | (zz == Z - 1)
+
+    def crosses(zz):
+        return (2 * z < Z) != (2 * zz < Z)
+
+    def p_send_inner(n):
+        for d in range(1, Z):
+            over = crosses(zoff(d)) & jnp.logical_not(inner)
+            first = (z == 0) & (zoff(d) == 1)
+            slot = jnp.where(over, 1, 0)
+
+            @pl.when(jnp.logical_not(outer(d) | first) & (slot == n))
+            def _():
+                p_copy(d).start()
+
+    for d in range(1, Z):
+        @pl.when(zoff(d) == 0)
+        def _():
+            p_copy(d).start()
+
+    with scope("side"):
+        @pl.when(x < X - 1)
+        def _():
+            pl.semaphore_wait(side, (X - 1 - x) * C)
     for h in range(H):
         for dx in range(1, X):
             remote(
@@ -107,35 +151,26 @@
                 dev(z, chip(dx), c),
             )
 
-    def p_block(zz, i, cc):
-        return all_p.at[zz, i, cc]
-
-    def p_copy(d):
-        zz = zoff(d)
-        cols = pl.ds(pl.multiple_of(zz * pb, pb), pb)
-        return copy(images.at[:, cols], p_block(z, 0, c), sent, p_recv.at[z, 0], dev(zz, x, c))
-
-    def outer(d):
-        zz = zoff(d)
-        return (zz == 0) | (zz == Z - 1)
-
-    def crosses(zz):
-        return (2 * z < Z) != (2 * zz < Z)
-
-    def p_send_inner(n):
+    def p_far(first):
+        @pl.loop(first, Z)
+        def _(zz):
+            pl.semaphore_wait(up.at[zz], 1)
+
         for d in range(1, Z):
-            over = crosses(zoff(d)) & jnp.logical_not(inner)
-            first = (z == 0) & (zoff(d) == 1)
-            slot = jnp.where(over, jnp.where(z == 0, 2, 1), 0)
-
-            @pl.when(jnp.logical_not(outer(d) | first) & (slot == n))
+            @pl.when(zoff(d) == Z - 1)
             def _():
                 p_copy(d).start()
 
-    for d in range(1, Z):
-        @pl.when(zoff(d) == 0)
-        def _():
-            p_copy(d).start()
+    with scope("up"):
+        if Z > 2:
+            @pl.when(z == 0)
+            def _():
+                pl.semaphore_wait(up.at[1], 1)
+                p_copy(1).start()
+
+            @pl.when(z > 0)
+            def _():
+                p_far(z + 1)
 
     with scope("small"):
         for cp in small:
@@ -168,27 +203,6 @@
             t = tmpl[rws, :].astype(jnp.float32)
             tnorm[rws, :] = jnp.broadcast_to(jnp.sum(t * t, axis=1, keepdims=True), (NORM, nb))
 
-    def p_far(first):
-        @pl.loop(first, Z)
-        def _(zz):
-            pl.semaphore_wait(up.at[zz], 1)
-
-        for d in range(1, Z):
-            @pl.when(zoff(d) == Z - 1)
-            def _():
-                p_copy(d).start()
-
-    with scope("up"):
-        if Z > 2:
-            @pl.when(z == 0)
-            def _():
-                pl.semaphore_wait(up.at[1], 1)
-                p_copy(1).start()
-
-            @pl.when(z > 0)
-            def _():
-                p_far(z + 1)
-
     def w_part(i, zz, q):
         return all_w.at[i, zz, pl.ds(q * gr, gr), :]
 
@@ -256,9 +270,6 @@
         own_stat[chip(i)] = jnp.where(row == 0, peak, total)
 
     def w_start(i):
-        if i == X - 1:
-            p_send_inner(2)
-
         if Z > 2:
             @pl.when(has_two)
             def _():
@@ -328,17 +339,19 @@
     p_send_inner(0)
 
     for dx in range(1, X):
-        for h in range(H):
+        for h in range(H // 2):
             gather(dx, h)
-            if h == H - 2:
-                for d in range(early, 1, -1):
-                    w_forwards(dx - 1, d, False)
-                    w_forwards(dx - 1, d, True, range(G - 1))
-                w_forwards(dx - 1, 1, False, range(G // 2))
-            elif h == H - 1:
-                for d in range(early, 1, -1):
-                    w_forwards(dx - 1, d, True, range(G - 1, G))
-                w_forwards(dx - 1, 1, False, range(G // 2, G))
+        for d in range(early, 1, -1):
+            w_forwards(dx - 1, d, False)
+        for h in range(H // 2, H - 1):
+            gather(dx, h)
+        for d in range(early, 1, -1):
+            w_forwards(dx - 1, d, True, range(G - 1))
+        w_forwards(dx - 1, 1, False, range(G // 2))
+        gather(dx, H - 1)
+        for d in range(early, 1, -1):
+            w_forwards(dx - 1, d, True, range(G - 1, G))
+        w_forwards(dx - 1, 1, False, range(G // 2, G))
         if dx == X - 1:
             p_send_inner(1)
             for d in range(1, early + 1):
@@ -383,14 +396,14 @@
     for d in range(1, Z):
         remote(fac.at[z], fac.at[z], sent, v_recv.at[z], dev(zoff(d), x, c))
 
-    def weights(zz, chunks, rws):
-        return jnp.concatenate(
-            [(all_w[i, zz, rws, :].astype(jnp.float32) * fac[zz, i, 0:1]).astype(jnp.bfloat16) for i in chunks], axis=1
-        )
-
-    def product(zz, chunks, rws):
-        block = all_p[zz, chunks[0] : chunks[-1] + 1].reshape(len(chunks) * nb, pb)
-        sums_ref[rws, :] += jnp.dot(weights(zz, chunks, rws), block, preferred_element_type=jnp.float32)
+    def near(fn, over):
+        def at(src, right):
+            ok = crosses(src) if over else jnp.logical_not(crosses(src))
+
+            @pl.when(ok)
+            def _():
+                fn(src, right)
+        sides(1, at)
 
     def second_step(src, right):
         for dx in range(1, X):
@@ -398,6 +411,15 @@
                 arrive(p_block(src, dx, c), p_recv.at[src, dx])
         for cp in p_second(src):
             cp.start()
+
+    def weights(zz, chunks, rws):
+        return jnp.concatenate(
+            [(all_w[i, zz, rws, :].astype(jnp.float32) * fac[zz, i, 0:1]).astype(jnp.bfloat16) for i in chunks], axis=1
+        )
+
+    def product(zz, chunks, rws):
+        block = all_p[zz, chunks[0] : chunks[-1] + 1].reshape(len(chunks) * nb, pb)
+        sums_ref[rws, :] += jnp.dot(weights(zz, chunks, rws), block, preferred_element_type=jnp.float32)
 
     def add_step(chunks):
         def fn(src, right):
@@ -424,6 +446,8 @@
     with scope("prod0"):
         sums_ref[...] = jnp.dot(weights(z, range(X), pl.ds(0, refs)), own_p, preferred_element_type=jnp.float32)
 
+    near(second_step, False)
+
     for d in range(early, 1, -1):
         p_slot(d, 2)
         w_forwards(X - 1, d, None)
@@ -435,20 +459,9 @@
         for i in range(X):
             w_forwards(i, d, None)
 
-    def near(fn, over):
-        def at(src, right):
-            ok = crosses(src) if over else jnp.logical_not(crosses(src))
-
-            @pl.when(ok)
-            def _():
-                fn(src, right)
-        sides(1, at)
-
     def lasts(d):
         for q in range(G):
             sides(d, last_step(q))
-
-    near(second_step, False)
 
     @pl.loop(2, Z)
     def _(d):
@@ -467,13 +480,15 @@
 
     @pl.when(jnp.logical_not(inner))
     def _():
-        @pl.loop(0, Z - 2)
-        def _(e):
-            sides(Z - 1 - e, add_step(range(max(X - 1, 1))))
+        @pl.loop(3, Z)
+        def _(d):
+            sides(d, add_step(range(X)))
+
+        if Z > 2:
+            sides(2, add_step(range(max(X - 1, 1))))
             if X > 1:
-                lasts(Z - 1 - e)
-
-        if Z == 2:
+                lasts(2)
+        else:
             near(add_step(range(X)), True)
 
     with scope("drain"):
@@ -561,7 +576,7 @@
             pltpu.VMEM((S, X, 8, nb), f32),
             pltpu.VMEM((Z, X, 8, nb), f32),
             dma((5,)), dma(()), dma(()), dma(()), dma((C,)), dma((X, H + C - 1)), dma((Z, X + C - 1)), dma((X, max(Z - 1, 1), G)), dma(()), dma((Z,)),
-            pltpu.SemaphoreType.REGULAR((Z,)),
+            pltpu.SemaphoreType.REGULAR((Z,)), pltpu.SemaphoreType.REGULAR,
         ],
         compiler_params=pltpu.CompilerParams(
             collective_id=0, has_side_effects=True, vmem_limit_bytes=56 * 1024 * 1024

time: 35.3 us -> 34.8 us (0.986)
  Pallas kernels: 34.5 us -> 34 us
    pallas_call x1, Pallas kernels: 33.2 us -> 32.6 us  [exchange(): pl.pallas_call(functools.partial(exchange_kernel, (Z, X, C, H, G)), out_s...]
where the time goes in v4:
time: 34.8 us; the launch traced here: 34.6 us
  Pallas kernels  34 us (98%)
  between operations  0.64 us (2%)
    pallas_call x1, Pallas kernels, exchange(): pl.pallas_call(functools.partial(exchange_kernel, (Z, X, C, H, G)), out_s...  32.6 us
    pallas_call x1, Pallas kernels, exchange(): pl.pallas_call(flush_kernel, out_shape=(jax.ShapeDtypeStruct((refs, pb),...  1.36 us

profile of v4, /device:TPU:0, one launch (start us, length us, event | category | flops | bytes accessed | tf_op | source)
XLA Modules:
  0.0 34.6 jit_solution(17008138318655616807)
XLA Ops:
  0.6 32.6 %shard_map.86 = (f32[512,1024]{1,0:T(8,128)S(1)}, f32[1,64]{1,0:T(1,128)S(1)}) custom-call(s32[2,1,128]{2,1,0:T(1,128)} %bitcast.2, f32[32]{0:T(128)} %ctf_in.1, f32[32]{0:T(128)} %prec_in.1, f32[128]{0:T(128)} %prior_in.1, s32[128]{0:T(128)} %mask_in.1, bf16[64,4096]{1,0:T(8,128)(2,1)} %images.1, bf16[512,4096]{1,0:T(8,128)(2,1)} %templates.1), custom_call_target="tpu_custom_call" | custom-call | tf_op jit(solution)/shard_map/pallas_call | solution.py:554
  33.3 1.4 %shard_map.87 = (f32[512,1024]{1,0:T(8,128)}, f32[1,64]{1,0:T(1,128)}) custom-call(f32[512,1024]{1,0:T(8,128)S(1)} %get-tuple-element.6.sums, f32[1,64]{1,0:T(1,128)S(1)} %get-tuple-element.7.evid), custom_call_target="tpu_custom_call" | custom-call | tf_op jit(solution)/shard_map/pallas_call | solution.py:585

commit v5 on v4

--- a/solution.py
+++ b/solution.py
@@ -10,6 +10,7 @@
 MASKED = -1e30
 PIECES = 4
 PARTS = 4
+LAST_PARTS = 8
 NORM = 64
 FLUSH = 4
 MESH = pl.DeviceIdType.MESH
@@ -21,7 +22,7 @@
     ids_ref, ctf_ref, prec_ref, prior_ref, mask_ref, grid_buf, tmpl, tnorm, base, act, all_w, all_p, own_stat, stat, fac,
     in_sem, tmpl_sem, own_sem, sent, c_recv, a_recv, p_recv, w_recv, s_recv, v_recv, up, side,
 ):
-    Z, X, C, H, G = sizes
+    Z, X, C, H, G, GL = sizes
     S = X * C
     g, z, x, c = [lax.axis_index(n) for n in ("groups", "img", "tpl", "sub")]
     refs, nb = tnorm.shape
@@ -29,7 +30,6 @@
     rows, pix = grid_buf.shape[2:]
     pb = pix // Z
     hr = rows // H
-    gr = refs // G
     s = x * C + c
 
     def chip(d):
@@ -43,6 +43,9 @@
 
     def dev(zz, xx, cc):
         return (g, zz, xx, cc)
+
+    def hop(src, dst):
+        return lax.rem(src - dst + Z - 1, Z)
 
     def scope(name):
         return jax.named_scope(name)
@@ -103,20 +106,20 @@
 
     @pl.loop(0, z)
     def _(zz):
-        pl.semaphore_signal(up.at[z], inc=1, device_id=dev(zz, x, c), device_id_type=MESH)
+        pl.semaphore_signal(up.at[jnp.where(zz == z - 1, 0, 1)], inc=1, device_id=dev(zz, x, c), device_id_type=MESH)
 
     def piece(i, cc, h):
         return grid_buf.at[i, cc, pl.ds(h * hr, hr), :]
 
     for dc in range(1, C):
-        remote(images, grid_buf.at[0, c], sent, c_recv.at[c], dev(z, x, core(dc)))
+        remote(images, grid_buf.at[0, c], sent, c_recv.at[C - dc - 1], dev(z, x, core(dc)))
     def p_block(zz, i, cc):
         return all_p.at[zz, i, cc]
 
     def p_copy(d):
         zz = zoff(d)
         cols = pl.ds(pl.multiple_of(zz * pb, pb), pb)
-        return copy(images.at[:, cols], p_block(z, 0, c), sent, p_recv.at[z, 0], dev(zz, x, c))
+        return copy(images.at[:, cols], p_block(z, 0, c), sent, p_recv.at[hop(z, zz), 0], dev(zz, x, c))
 
     def outer(d):
         zz = zoff(d)
@@ -147,14 +150,19 @@
     for h in range(H):
         for dx in range(1, X):
             remote(
-                images.at[pl.ds(h * hr, hr), :], piece(X - dx, c, h), sent, a_recv.at[X - dx, h],
+                images.at[pl.ds(h * hr, hr), :], piece(X - dx, c, h), sent, a_recv.at[X - dx - 1, h],
                 dev(z, chip(dx), c),
             )
 
-    def p_far(first):
-        @pl.loop(first, Z)
-        def _(zz):
-            pl.semaphore_wait(up.at[zz], 1)
+    def wait_next():
+        @pl.when(z < Z - 1)
+        def _():
+            pl.semaphore_wait(up.at[0], 1)
+
+    def p_far():
+        @pl.when(z < Z - 2)
+        def _():
+            pl.semaphore_wait(up.at[1], Z - 2 - z)
 
         for d in range(1, Z):
             @pl.when(zoff(d) == Z - 1)
@@ -165,12 +173,13 @@
         if Z > 2:
             @pl.when(z == 0)
             def _():
-                pl.semaphore_wait(up.at[1], 1)
+                wait_next()
                 p_copy(1).start()
 
             @pl.when(z > 0)
             def _():
-                p_far(z + 1)
+                wait_next()
+                p_far()
 
     with scope("small"):
         for cp in small:
@@ -203,11 +212,15 @@
             t = tmpl[rws, :].astype(jnp.float32)
             tnorm[rws, :] = jnp.broadcast_to(jnp.sum(t * t, axis=1, keepdims=True), (NORM, nb))
 
+    def count(i):
+        return GL if i == X - 1 else G
+
     def w_part(i, zz, q):
-        return all_w.at[i, zz, pl.ds(q * gr, gr), :]
+        n = refs // count(i)
+        return all_w.at[i, zz, pl.ds(q * n, n), :]
 
     def w_sem(i, src, dst, q):
-        return w_recv.at[i, lax.rem(src - dst + Z - 1, Z), q]
+        return w_recv.at[hop(src, dst), i * G + q]
 
     def w_go(i, zz, q, right):
         to = lax.rem(z + (1 if right else -1) + Z, Z)
@@ -242,10 +255,10 @@
                 w_go(i, src, q, right).start()
         return fn
 
-    def w_forwards(i, d, side, parts=range(G)):
+    def w_forwards(i, d, side, parts=None):
         def fn(src, right):
             if side is None or side == right:
-                for q in parts:
+                for q in parts or range(count(i)):
                     w_forward(i, q)(src, right)
         sides(d, fn)
 
@@ -273,10 +286,10 @@
         if Z > 2:
             @pl.when(has_two)
             def _():
-                for q in range(G):
+                for q in range(count(i)):
                     w_two(i, q).start()
 
-        for q in range(G):
+        for q in range(count(i)):
             @pl.when(z < Z - 1)
             def _():
                 w_go(i, z, q, True).start()
@@ -288,21 +301,21 @@
     def p_forward(zz):
         out = []
         for dx in range(1, X):
-            out.append(copy(p_block(zz, 0, c), p_block(zz, X - dx, c), sent, p_recv.at[zz, X - dx], dev(z, chip(dx), c)))
+            out.append(copy(p_block(zz, 0, c), p_block(zz, X - dx, c), sent, p_recv.at[hop(zz, z), X - dx], dev(z, chip(dx), c)))
         for dc in range(1, C):
-            out.append(copy(p_block(zz, 0, c), p_block(zz, 0, c), sent, p_recv.at[zz, X + C - 1 - dc], dev(z, x, core(dc))))
+            out.append(copy(p_block(zz, 0, c), p_block(zz, 0, c), sent, p_recv.at[hop(zz, z), X + C - 1 - dc], dev(z, x, core(dc))))
         return out
 
     def p_second(zz):
         out = []
         for dx in range(1, X):
             for dc in range(1, C):
-                out.append(copy(p_block(zz, dx, c), p_block(zz, dx, c), sent, p_recv.at[zz, X + C - 1 - dc], dev(z, x, core(dc))))
+                out.append(copy(p_block(zz, dx, c), p_block(zz, dx, c), sent, p_recv.at[hop(zz, z), X + C - 1 - dc], dev(z, x, core(dc))))
         return out
 
     def p_start(zz, right):
         with scope("pst"):
-            arrive(p_block(zz, 0, c), p_recv.at[zz, 0])
+            arrive(p_block(zz, 0, c), p_recv.at[hop(zz, z), 0])
         for cp in p_forward(zz):
             cp.start()
 
@@ -318,20 +331,22 @@
 
     def gather(dx, h):
         with scope(f"gath{h}"):
-            arrive(piece(dx, c, h), a_recv.at[dx, h])
+            arrive(piece(dx, c, h), a_recv.at[dx - 1, h])
         for dc in range(1, C):
-            remote(piece(dx, c, h), piece(dx, c, h), sent, a_recv.at[dx, H + C - 1 - dc], dev(z, x, core(dc)))
+            remote(piece(dx, c, h), piece(dx, c, h), sent, a_recv.at[dx - 1, H + C - 1 - dc], dev(z, x, core(dc)))
 
     own_copy.wait()
     with scope("own"):
         for dc in range(1, C):
-            arrive(grid_buf.at[0, core(dc)], c_recv.at[core(dc)])
+            arrive(grid_buf.at[0, core(dc)], c_recv.at[dc - 1])
     with scope("sc0"):
         scores(0)
 
     @pl.when(z == 0)
     def _():
-        p_far(min(2, Z - 1))
+        if Z == 2:
+            wait_next()
+        p_far()
 
     w_start(0)
     if X == 1:
@@ -358,7 +373,7 @@
                 p_slot(d, 0)
         with scope(f"arrA{dx}"):
             for dc in range(1, C):
-                arrive(grid_buf.at[dx, core(dc)], a_recv.at[dx, H + dc - 1])
+                arrive(grid_buf.at[dx, core(dc)], a_recv.at[dx - 1, H + dc - 1])
         with scope(f"sc{dx}"):
             scores(dx)
         w_start(dx)
@@ -394,7 +409,7 @@
                 mine = jnp.where(c == q, evid[:, q * rows : (q + 1) * rows], mine)
             evid_ref[...] = mine
     for d in range(1, Z):
-        remote(fac.at[z], fac.at[z], sent, v_recv.at[z], dev(zoff(d), x, c))
+        remote(fac.at[z], fac.at[z], sent, v_recv.at[Z - d - 1], dev(zoff(d), x, c))
 
     def near(fn, over):
         def at(src, right):
@@ -408,7 +423,7 @@
     def second_step(src, right):
         for dx in range(1, X):
             with scope("psec"):
-                arrive(p_block(src, dx, c), p_recv.at[src, dx])
+                arrive(p_block(src, dx, c), p_recv.at[hop(src, z), dx])
         for cp in p_second(src):
             cp.start()
 
@@ -424,13 +439,13 @@
     def add_step(chunks):
         def fn(src, right):
             for i in chunks:
-                for q in range(G):
+                for q in range(count(i)):
                     w_wait(i, q)(src, right)
             with scope("vw"):
-                arrive(fac.at[src], v_recv.at[src])
+                arrive(fac.at[src], v_recv.at[hop(src, z)])
             with scope("addw"):
                 for dc in range(1, C):
-                    arrive(all_p.at[src, :, core(dc)], p_recv.at[src, X + dc - 1])
+                    arrive(all_p.at[src, :, core(dc)], p_recv.at[hop(src, z), X + dc - 1])
             with scope("addp"):
                 product(src, chunks, pl.ds(0, refs))
         return fn
@@ -439,7 +454,7 @@
         def fn(src, right):
             w_wait(X - 1, q)(src, right)
             with scope(f"last{q}"):
-                product(src, range(X - 1, X), pl.ds(q * gr, gr))
+                product(src, range(X - 1, X), pl.ds(q * (refs // GL), refs // GL))
         return fn
 
     own_p = grid_buf[:, :, :, pl.ds(pl.multiple_of(z * pb, pb), pb)].reshape(X * nb, pb)
@@ -460,7 +475,7 @@
             w_forwards(i, d, None)
 
     def lasts(d):
-        for q in range(G):
+        for q in range(GL):
             sides(d, last_step(q))
 
     @pl.loop(2, Z)
@@ -503,7 +518,7 @@
             for i in range(X):
                 @pl.when(forwards(src, right))
                 def _():
-                    for q in range(G):
+                    for q in range(count(i)):
                         w_go(i, src, q, right).wait_send()
 
         @pl.loop(1, Z)
@@ -511,7 +526,7 @@
             sides(d, end_step)
 
         for i in range(X):
-            for q in range(G):
+            for q in range(count(i)):
                 if Z > 2:
                     @pl.when(has_two)
                     def _():
@@ -546,13 +561,13 @@
     refs = templates.shape[0]
     nb = C * rows
     pb = pix // Z
-    H, G = PIECES, PARTS
+    H, G, GL = PIECES, PARTS, LAST_PARTS
     vmem = pl.BlockSpec(memory_space=pltpu.VMEM)
     anyw = pl.BlockSpec(memory_space=pl.ANY)
     dma = pltpu.SemaphoreType.DMA
     f32, bf16 = jnp.float32, jnp.bfloat16
     class_sums, evid = pl.pallas_call(
-        functools.partial(exchange_kernel, (Z, X, C, H, G)),
+        functools.partial(exchange_kernel, (Z, X, C, H, G, GL)),
         out_shape=(
             pltpu.VMEM((refs, pb), f32),
             pltpu.VMEM((1, rows), f32),
@@ -575,8 +590,8 @@
             pltpu.VMEM((X, 8, nb), f32),
             pltpu.VMEM((S, X, 8, nb), f32),
             pltpu.VMEM((Z, X, 8, nb), f32),
-            dma((5,)), dma(()), dma(()), dma(()), dma((C,)), dma((X, H + C - 1)), dma((Z, X + C - 1)), dma((X, max(Z - 1, 1), G)), dma(()), dma((Z,)),
-            pltpu.SemaphoreType.REGULAR((Z,)), pltpu.SemaphoreType.REGULAR,
+            dma((5,)), dma(()), dma(()), dma(()), dma((max(C - 1, 1),)), dma((max(X - 1, 1), H + C - 1)), dma((max(Z - 1, 1), X + C - 1)), dma((max(Z - 1, 1), (X - 1) * G + GL)), dma(()), dma((max(Z - 1, 1),)),
+            pltpu.SemaphoreType.REGULAR((2,)), pltpu.SemaphoreType.REGULAR,
         ],
         compiler_params=pltpu.CompilerParams(
             collective_id=0, has_side_effects=True, vmem_limit_bytes=56 * 1024 * 1024

time: 34.8 us -> 34.6 us (level)
  no operation moved by 1% of the time
where the time goes in v5:
time: 34.6 us; the launch traced here: 34.5 us
  Pallas kernels  33.9 us (98%)
  between operations  0.64 us (2%)
    pallas_call x1, Pallas kernels, exchange(): pl.pallas_call(functools.partial(exchange_kernel, (Z, X, C, H, G, GL)), o...  32.5 us
    pallas_call x1, Pallas kernels, exchange(): pl.pallas_call(flush_kernel, out_shape=(jax.ShapeDtypeStruct((refs, pb),...  1.36 us

profile of v5, /device:TPU:0, one launch (start us, length us, event | category | flops | bytes accessed | tf_op | source)
XLA Modules:
  0.0 34.5 jit_solution(1049106912741050520)
XLA Ops:
  0.6 32.5 %shard_map.86 = (f32[512,1024]{1,0:T(8,128)S(1)}, f32[1,64]{1,0:T(1,128)S(1)}) custom-call(s32[2,1,128]{2,1,0:T(1,128)} %bitcast.2, f32[32]{0:T(128)} %ctf_in.1, f32[32]{0:T(128)} %prec_in.1, f32[128]{0:T(128)} %prior_in.1, s32[128]{0:T(128)} %mask_in.1, bf16[64,4096]{1,0:T(8,128)(2,1)} %images.1, bf16[512,4096]{1,0:T(8,128)(2,1)} %templates.1), custom_call_target="tpu_custom_call" | custom-call | tf_op jit(solution)/shard_map/pallas_call | solution.py:569
  33.1 1.4 %shard_map.87 = (f32[512,1024]{1,0:T(8,128)}, f32[1,64]{1,0:T(1,128)}) custom-call(f32[512,1024]{1,0:T(8,128)S(1)} %get-tuple-element.6.sums, f32[1,64]{1,0:T(1,128)S(1)} %get-tuple-element.7.evid), custom_call_target="tpu_custom_call" | custom-call | tf_op jit(solution)/shard_map/pallas_call | solution.py:600

commit v6 on v5

--- a/solution.py
+++ b/solution.py
@@ -9,7 +9,7 @@
 ROTS = 16
 MASKED = -1e30
 PIECES = 4
-PARTS = 4
+PARTS = 2
 LAST_PARTS = 8
 NORM = 64
 FLUSH = 4
@@ -457,16 +457,17 @@
                 product(src, range(X - 1, X), pl.ds(q * (refs // GL), refs // GL))
         return fn
 
-    own_p = grid_buf[:, :, :, pl.ds(pl.multiple_of(z * pb, pb), pb)].reshape(X * nb, pb)
-    with scope("prod0"):
-        sums_ref[...] = jnp.dot(weights(z, range(X), pl.ds(0, refs)), own_p, preferred_element_type=jnp.float32)
-
     near(second_step, False)
 
     for d in range(early, 1, -1):
         p_slot(d, 2)
         w_forwards(X - 1, d, None)
     p_slot(1, 3)
+
+    own_p = grid_buf[:, :, :, pl.ds(pl.multiple_of(z * pb, pb), pb)].reshape(X * nb, pb)
+    with scope("prod0"):
+        sums_ref[...] = jnp.dot(weights(z, range(X), pl.ds(0, refs)), own_p, preferred_element_type=jnp.float32)
+
     w_forwards(X - 1, 1, None)
 
     @pl.loop(early + 1, Z)

time: 34.6 us -> 34.4 us (level)
  no operation moved by 1% of the time
where the time goes in v6:
time: 34.4 us; the launch traced here: 34.3 us
  Pallas kernels  33.6 us (98%)
  between operations  0.64 us (2%)
    pallas_call x1, Pallas kernels, exchange(): pl.pallas_call(functools.partial(exchange_kernel, (Z, X, C, H, G, GL)), o...  32.3 us
    pallas_call x1, Pallas kernels, exchange(): pl.pallas_call(flush_kernel, out_shape=(jax.ShapeDtypeStruct((refs, pb),...  1.36 us

profile of v6, /device:TPU:0, one launch (start us, length us, event | category | flops | bytes accessed | tf_op | source)
XLA Modules:
  0.0 34.3 jit_solution(13115053204009695608)
XLA Ops:
  0.6 32.3 %shard_map.86 = (f32[512,1024]{1,0:T(8,128)S(1)}, f32[1,64]{1,0:T(1,128)S(1)}) custom-call(s32[2,1,128]{2,1,0:T(1,128)} %bitcast.2, f32[32]{0:T(128)} %ctf_in.1, f32[32]{0:T(128)} %prec_in.1, f32[128]{0:T(128)} %prior_in.1, s32[128]{0:T(128)} %mask_in.1, bf16[64,4096]{1,0:T(8,128)(2,1)} %images.1, bf16[512,4096]{1,0:T(8,128)(2,1)} %templates.1), custom_call_target="tpu_custom_call" | custom-call | tf_op jit(solution)/shard_map/pallas_call | solution.py:570
  32.9 1.4 %shard_map.87 = (f32[512,1024]{1,0:T(8,128)}, f32[1,64]{1,0:T(1,128)}) custom-call(f32[512,1024]{1,0:T(8,128)S(1)} %get-tuple-element.6.sums, f32[1,64]{1,0:T(1,128)S(1)} %get-tuple-element.7.evid), custom_call_target="tpu_custom_call" | custom-call | tf_op jit(solution)/shard_map/pallas_call | solution.py:601

commit v7 on v6

--- a/solution.py
+++ b/solution.py
@@ -11,8 +11,8 @@
 PIECES = 4
 PARTS = 2
 LAST_PARTS = 8
-NORM = 64
-FLUSH = 4
+NORM = 128
+FLUSH = 1
 MESH = pl.DeviceIdType.MESH
 
 

time: 34.4 us -> 34.6 us (level)
  no operation moved by 1% of the time
where the time goes in v7:
time: 34.6 us; the launch traced here: 34.3 us
  Pallas kernels  33.6 us (97%)
  between operations  0.64 us (2%)
    pallas_call x1, Pallas kernels, exchange(): pl.pallas_call(functools.partial(exchange_kernel, (Z, X, C, H, G, GL)), o...  32.3 us
    pallas_call x1, Pallas kernels, exchange(): pl.pallas_call(flush_kernel, out_shape=(jax.ShapeDtypeStruct((refs, pb),...  1.34 us

profile of v7, /device:TPU:0, one launch (start us, length us, event | category | flops | bytes accessed | tf_op | source)
XLA Modules:
  0.0 34.3 jit_solution(7948363982809855444)
XLA Ops:
  0.6 32.3 %shard_map.86 = (f32[512,1024]{1,0:T(8,128)S(1)}, f32[1,64]{1,0:T(1,128)S(1)}) custom-call(s32[2,1,128]{2,1,0:T(1,128)} %bitcast.2, f32[32]{0:T(128)} %ctf_in.1, f32[32]{0:T(128)} %prec_in.1, f32[128]{0:T(128)} %prior_in.1, s32[128]{0:T(128)} %mask_in.1, bf16[64,4096]{1,0:T(8,128)(2,1)} %images.1, bf16[512,4096]{1,0:T(8,128)(2,1)} %templates.1), custom_call_target="tpu_custom_call" | custom-call | tf_op jit(solution)/shard_map/pallas_call | solution.py:570
  32.9 1.3 %shard_map.87 = (f32[512,1024]{1,0:T(8,128)}, f32[1,64]{1,0:T(1,128)}) custom-call(f32[512,1024]{1,0:T(8,128)S(1)} %get-tuple-element.6.sums, f32[1,64]{1,0:T(1,128)S(1)} %get-tuple-element.7.evid), custom_call_target="tpu_custom_call" | custom-call | tf_op jit(solution)/shard_map/pallas_call | solution.py:601
